TPU v7x, 32 devices: a whole 2x2x4 slice. The times are simulated.
32 devices in a mesh: gy: 8 (over z, core), gx: 4 (over y, x).
Axes of the slice: x: 2, y: 2, z: 4, core: 2. Of those that a mesh axis runs over, the one named last changes fastest.
Arguments:
- mean_util: float32 [32, 64, 128], P(None, 'gy', 'gx'), may hold values from -4 to 4
- observed_shares: float32 [32, 64, 128], P(None, 'gy', 'gx'), may hold values from 0.002 to 0.02
- characteristics: float32 [4, 32, 64, 128], P(None, None, 'gy', 'gx'), may hold values from -2 to 2
- taste_draws: float32 [4, 512], replicated, may hold values from -4 to 4
- taste_scale: float32 [4], replicated, may hold values from 0.3 to 1
- prior_probs: bfloat16 [32, 64, 128, 512], P(None, 'gy', 'gx'), may hold values from 0 to 0.099609375
- spill_rate: float32 [32], replicated, may hold values from 1 to 8
- utility_rate: float32 [32], replicated, may hold values from 0.1 to 0.6
- adjacency: int32 [4, 64, 128], P(None, 'gy', 'gx'), may hold values from 0 to 3
Outputs:
- final_util: float32 [32, 64, 128], P(None, 'gy', 'gx')
- log_shares: float32 [32, 64, 128], P(None, 'gy', 'gx')
- residual_max: float32 [3], replicated
All inputs are finite; a program needn't handle non-finite values. Where the computation divides by a largest or mean magnitude, that divisor is 1e-20 or more.
Results may differ from a plain program's by a relative error of at most 0.0008.
Values may be sent and summed in bfloat16 or wider, within the bound.
No kernel may reach another device: no remote copies, remote signals or barrier semaphores. Data moves between devices by JAX's collectives and lax.ppermute only.
A program may use at most 192 MiB of HBM per device.

v0:
```python
import functools
import math

import jax
import jax.numpy as jnp
from jax import lax
from jax.experimental import pallas as pl
from jax.experimental.pallas import tpu as pltpu
from jax.sharding import PartitionSpec as P

ITERS = 3
step_level = 0.2
gap_eps = 1e-06
LANES = 128
GROUP = 4
F32 = jnp.float32
BF16 = jnp.bfloat16
LOG2E = 1.0 / math.log(2.0)


def rounded(x):
    return lax.reduce_precision(x, 8, 7)


def split_parts(x, count):
    parts = []
    for _ in range(count):
        part = rounded(x)
        parts.append(part.astype(BF16))
        x = x - part
    return parts


def kernel_parts(x, count):
    parts = []
    for _ in range(count):
        part = x.astype(BF16)
        parts.append(part)
        x = x - part.astype(F32)
    return parts


def dot(a, b):
    return jnp.dot(a, b, preferred_element_type=F32)


def step_kernel(dims, first, last, *refs):
    J, TR, TC, R, ND = dims
    M = TR * TC
    LO = LANES - J
    refs = list(refs)
    parity = refs.pop(0)
    spill = refs.pop(0)
    if not first:
        mall, res_in, mh_in = refs[:3]
        refs = refs[3:]
    mean_in, state, hB, hA, hC, hD, Wl, Wc, T4, dsel, cnt, rate, ispill, logobs = refs[:14]
    refs = refs[14:]
    if last:
        mean_out, res_out, log_out, mloc = refs[:4]
        refs = refs[4:]
    else:
        state_out, pB, pA, pC, pD, mean_out, res_out, mh_out, mloc = refs[:9]
        refs = refs[9:]
    E, den, Wcb, W4b, S_ref, sc_ref = refs[:6]
    if not last:
        colf = refs[6]

    rim = []
    for h in (hB, hA, hC, hD):
        rim.append(h[J, :, 0:LANES].astype(F32) + h[J, :, LANES : 2 * LANES].astype(F32))
    rim.append(jnp.zeros((LANES - 2 * (TR + TC), LANES), F32))
    rim = jnp.concatenate(rim, axis=0)
    if first:
        mean = mean_in[...]
        mh = rim
    else:
        step = step_level / (jnp.max(mall[...]) + gap_eps)
        mean = mean_in[...] + step * res_in[...]
        mh = mh_in[...] + step * rim
    mean_out[...] = mean
    if not last:
        mh_out[...] = mh
    acc = jnp.zeros((M, LANES), F32)
    for part in kernel_parts(mean, 3):
        acc = acc + dot(Wl[...], part)
    for part in kernel_parts(mh, 3):
        acc = acc + dot(Wc[...], part)
    scaled = (mean * cnt[...] + rate[...] * acc) * ispill[...]
    b_hi, b_mid = kernel_parts(scaled, 2)
    Wcb[...] = Wc[...] + b_hi
    for g in range(J // GROUP):
        W4b[g] = T4[g] + b_mid
    sc_ref[...] = LOG2E / cnt[...]
    den[...] = jnp.ones_like(den)

    row_id = lax.broadcasted_iota(jnp.int32, (J, R), 0)
    zeros_mid = jnp.zeros((LO - 2 * (TR + TC), R), BF16)

    def pass_one(g, carry):
        for q in range(GROUP):
            j = g * GROUP + q
            onehot = jnp.where(row_id == j, 1.0, 0.0).astype(BF16)
            cd = jnp.concatenate([hC[j].astype(F32), hD[j].astype(F32)], axis=0).astype(BF16)
            rhs = jnp.concatenate([hB[j], hA[j], cd, zeros_mid, onehot, dsel[q], onehot], axis=0)
            lhs = jnp.concatenate([Wcb[...], W4b[g]], axis=1)
            total = dot(Wl[...], state[j]) + dot(lhs, rhs)
            factor = sc_ref[...] * spill[j]
            factor = jnp.concatenate([factor] * (R // LANES), axis=1)
            e = jnp.exp2(total * factor)
            E[j] = e
            den[...] += e
        return carry

    lax.fori_loop(0, J // GROUP, pass_one, 0)
    den[...] = 1.0 / den[...]

    lane = lax.broadcasted_iota(jnp.int32, (TC, LANES), 1)

    def chunk(mc, carry):
        rows = pl.ds(pl.multiple_of(mc * TC, TC), TC)

        def pass_two(g, sums):
            inverse = den[rows, :]
            for q in range(GROUP):
                j = g * GROUP + q
                prob = E[j, rows, :] * inverse
                if not last:
                    state_out[j, rows, :] = prob.astype(BF16)
                    colf[0, j, pl.ds(mc, 1), :] = prob[0:1]
                    colf[1, j, pl.ds(mc, 1), :] = prob[TC - 1 : TC]
                part = prob[:, 0:LANES]
                for b in range(1, R // LANES):
                    part = part + prob[:, b * LANES : (b + 1) * LANES]
                total = jnp.sum(part, axis=1, keepdims=True)
                sums = jnp.where(lane == LO + j, total, sums)
            return sums

        S_ref[rows, :] = lax.fori_loop(0, J // GROUP, pass_two, jnp.zeros((TC, LANES), F32))
        return carry

    lax.fori_loop(0, TR, chunk, 0)

    full_lane = lax.broadcasted_iota(jnp.int32, (M, LANES), 1)
    log_pred = jnp.log(S_ref[...] * (1.0 / R))
    res = jnp.where(full_lane >= LO, logobs[...] - log_pred, 0.0)
    res_out[...] = res
    mloc[...] = jnp.broadcast_to(jnp.max(jnp.abs(res)), (ND, LANES))
    if last:
        log_out[...] = log_pred
        return

    py = parity[0]
    px = parity[1]

    def plane(ref, values):
        hi, mid = kernel_parts(values, 2)
        ref[J, :, 0:LANES] = hi
        ref[J, :, LANES : 2 * LANES] = mid
        ref[J, :, 2 * LANES :] = jnp.zeros((values.shape[0], R - 2 * LANES), BF16)

    for ref, start in ((pB, py * (M - TC)), (pA, (1 - py) * (M - TC))):
        rows = pl.ds(pl.multiple_of(start, TC), TC)
        plane(ref, res_out[rows, :])

        def copy_rows(j, carry, ref=ref, rows=rows):
            ref[j] = state_out[j, rows, :]
            return carry

        lax.fori_loop(0, J, copy_rows, 0)
    west = res_out[pl.ds(0, TR, stride=TC), :]
    east = res_out[pl.ds(TC - 1, TR, stride=TC), :]
    plane(pC, jnp.where(px == 0, east, west))
    plane(pD, jnp.where(px == 0, west, east))

    def copy_cols(j, carry):
        pC[j] = colf[1 - px, j].astype(BF16)
        pD[j] = colf[px, j].astype(BF16)
        return carry

    lax.fori_loop(0, J, copy_cols, 0)


def run_step(dims, first, last, *args):
    J, TR, TC, R, ND = dims
    M = TR * TC
    smem = pl.BlockSpec(memory_space=pltpu.SMEM)
    vmem = pl.BlockSpec(memory_space=pltpu.VMEM)
    table = jax.ShapeDtypeStruct((M, LANES), F32)
    peak = jax.ShapeDtypeStruct((ND, LANES), F32)
    if last:
        out_shape = (table, table, table, peak)
    else:
        row = jax.ShapeDtypeStruct((J + 1, TC, R), BF16)
        col = jax.ShapeDtypeStruct((J + 1, TR, R), BF16)
        halo = jax.ShapeDtypeStruct((LANES, LANES), F32)
        state = jax.ShapeDtypeStruct((J, M, R), BF16)
        out_shape = (state, row, row, col, col, table, table, halo, peak)
    scratch = [
        pltpu.VMEM((J, M, R), F32),
        pltpu.VMEM((M, R), F32),
        pltpu.VMEM((M, LANES), BF16),
        pltpu.VMEM((J // GROUP, M, LANES), BF16),
        pltpu.VMEM((M, LANES), F32),
        pltpu.VMEM((M, LANES), F32),
    ]
    if not last:
        scratch.append(pltpu.VMEM((2, J, TR, R), F32))
    return pl.pallas_call(
        functools.partial(step_kernel, dims, first, last),
        out_shape=out_shape,
        in_specs=[smem, smem] + [vmem] * (len(args) - 2),
        out_specs=tuple(vmem for _ in out_shape),
        scratch_shapes=scratch,
        compiler_params=pltpu.CompilerParams(vmem_limit_bytes=56 * 1024 * 1024),
        name="first_step" if first else ("last_step" if last else "mid_step"),
    )(*args)


def pair_perms(size):
    near = [(i, i ^ 1) for i in range(size) if (i ^ 1) < size]
    far = [(i, i + 1 if i % 2 else i - 1) for i in range(size)]
    far = [(i, k) for i, k in far if 0 <= k < size]
    return near, far


def local(
    mean_util,
    observed_shares,
    characteristics,
    taste_draws,
    taste_scale,
    prior_probs,
    spill_rate,
    utility_rate,
    adjacency,
):
    J, TR, TC = mean_util.shape
    K, R = taste_draws.shape
    M = TR * TC
    LO = LANES - J
    ny, nx = lax.axis_size("gy"), lax.axis_size("gx")
    dims = (J, TR, TC, R, ny * nx)
    py = lax.axis_index("gy") % 2
    px = lax.axis_index("gx") % 2
    near_y, far_y = pair_perms(ny)
    near_x, far_x = pair_perms(nx)

    def exchange(pB, pA, pC, pD):
        return (
            lax.ppermute(pB, "gy", far_y),
            lax.ppermute(pA, "gy", near_y),
            lax.ppermute(pC, "gx", near_x),
            lax.ppermute(pD, "gx", far_x),
        )

    def first_payload(index, axis):
        state = lax.dynamic_index_in_dim(prior_probs, index, axis, keepdims=False)
        mean = lax.dynamic_index_in_dim(mean_util, index, axis, keepdims=False).T
        parts = [jnp.pad(p, ((0, 0), (LO, 0))) for p in split_parts(mean, 2)]
        tail = jnp.zeros((mean.shape[0], R - 2 * LANES), BF16)
        plane = jnp.concatenate(parts + [tail], axis=1)
        return jnp.concatenate([state, plane[None]], axis=0)

    row_b, row_a = py * (TR - 1), (1 - py) * (TR - 1)
    col_c, col_d = (1 - px) * (TC - 1), px * (TC - 1)
    halos = exchange(
        first_payload(row_b, 1), first_payload(row_a, 1), first_payload(col_c, 2), first_payload(col_d, 2)
    )

    def table(x):
        return jnp.pad(x.reshape(J, M).T, ((0, 0), (LO, 0)))

    links = adjacency.astype(F32).reshape(4, M, 1)
    count = jnp.maximum(jnp.sum(links, axis=0), 1.0)
    me = lax.broadcasted_iota(jnp.int32, (M, M), 0)
    other = lax.broadcasted_iota(jnp.int32, (M, M), 1)
    my_col = me % TC
    Wl = (
        jnp.where(other == me - TC, links[0], 0.0)
        + jnp.where(other == me + TC, links[1], 0.0)
        + jnp.where((other == me - 1) & (my_col > 0), links[2], 0.0)
        + jnp.where((other == me + 1) & (my_col < TC - 1), links[3], 0.0)
    ).astype(BF16)
    mrow = lax.broadcasted_iota(jnp.int32, (M, LANES), 0)
    lane = lax.broadcasted_iota(jnp.int32, (M, LANES), 1)
    r, c = mrow // TC, mrow % TC
    north = jnp.where(r == 0, links[0], 0.0)
    south = jnp.where(r == TR - 1, links[1], 0.0)
    west = jnp.where(c == 0, links[2], 0.0)
    east = jnp.where(c == TC - 1, links[3], 0.0)
    Wc = (
        jnp.where(lane == c, jnp.where(py == 1, south, north), 0.0)
        + jnp.where(lane == TC + c, jnp.where(py == 1, north, south), 0.0)
        + jnp.where(lane == 2 * TC + r, jnp.where(px == 1, west, east), 0.0)
        + jnp.where(lane == 2 * TC + TR + r, jnp.where(px == 1, east, west), 0.0)
    ).astype(BF16)
    cnt = jnp.broadcast_to(count, (M, LANES))

    per_rate = taste_scale[None, :] / spill_rate[:, None]
    taste = characteristics.reshape(K, J, M).transpose(2, 1, 0) * per_rate[None] * count[:, :, None]
    c_hi, c_mid, c_lo = split_parts(taste, 3)
    d_hi, d_mid, d_lo = split_parts(taste_draws, 3)
    lefts = (c_hi, c_hi, c_mid, c_hi, c_mid, c_lo)
    rights = (d_hi, d_mid, d_hi, d_lo, d_mid, d_hi)
    width = GROUP * K
    groups = J // GROUP
    lefts = [x.reshape(M, groups, width).transpose(1, 0, 2) for x in lefts]
    T4 = jnp.concatenate(lefts, axis=2)
    T4 = jnp.pad(T4, ((0, 0), (0, 0), (0, LANES - T4.shape[2])))
    eye = jnp.eye(GROUP, dtype=BF16)
    rights = [(eye[:, :, None, None] * x[None, None]).reshape(GROUP, width, R) for x in rights]
    dsel = jnp.concatenate(rights, axis=1)
    dsel = jnp.pad(dsel, ((0, 0), (0, LO - dsel.shape[1]), (0, 0)))

    rate = jnp.pad(utility_rate[None], ((0, 0), (LO, 0)))
    ispill = jnp.pad((1.0 / spill_rate)[None], ((0, 0), (LO, 0)))
    logobs = jnp.pad(jnp.log(observed_shares).reshape(J, M).T, ((0, 0), (LO, 0)))
    parity = jnp.stack([py, px]).astype(jnp.int32)
    fixed = (Wl, Wc, T4, dsel, cnt, rate, ispill, logobs)

    mean = table(mean_util)
    state = prior_probs.reshape(J, M, R)
    peaks = []
    res = rim = None
    for iteration in range(ITERS):
        first, last = iteration == 0, iteration + 1 == ITERS
        moving = () if first else (peaks[-1], res, rim)
        args = (parity, spill_rate) + moving + (mean, state) + halos + fixed
        out = run_step(dims, first, last, *args)
        if last:
            mean, res, log_pred, peak = out
        else:
            state, pB, pA, pC, pD, mean, res, rim, peak = out
            halos = exchange(pB, pA, pC, pD)
        peaks.append(lax.all_to_all(peak, ("gy", "gx"), 0, 0, tiled=True))
    worst = jnp.stack([jnp.max(p) for p in peaks])
    step = step_level / (worst[-1] + gap_eps)

    def untable(x):
        return x[:, LO:].T.reshape(J, TR, TC)

    return untable(mean + step * res), untable(log_pred), worst


def solution(mesh):
    placed = (
        P(None, "gy", "gx"),
        P(None, "gy", "gx"),
        P(None, None, "gy", "gx"),
        P(),
        P(),
        P(None, "gy", "gx", None),
        P(),
        P(),
        P(None, "gy", "gx"),
    )
    return jax.shard_map(
        local,
        mesh=mesh,
        in_specs=placed,
        out_specs=(P(None, "gy", "gx"), P(None, "gy", "gx"), P()),
        check_vma=False,
    )
```

profile of v0, /device:TPU:0, one launch (start us, length us, event | category | flops | bytes accessed | tf_op | source)
XLA Modules:
  0.0 152.5 jit_solution(9473327589215745181)
XLA Ops:
  0.7 1.7 %dynamic-slice_bitcast_fusion = (bf16[32,32,512]{2,1,0:T(8,128)(2,1)S(1)}, bf16[32,32,512]{2,1,0:T(8,128)(2,1)S(1)}) fusion(bf16[32,8,32,512]{3,2,1,0:T(8,128)(2,1)} %param.14, s32[]{:T(128)S(6)} %select_n.126, s32[]{:T(128)S(6)} %select_n.125), kind=kLoop, calls=%fused_computation.2 | loop fusion | bytes 4194312 | tf_op jit(solution)/shard_map/jit(dynamic_index_in_dim)/squeeze | solution.py:258
  2.7 1.1 pad_maximum_fusion.1
  3.8 0.5 collective-permute-start.1
  4.3 1.1 pad_maximum_fusion
  5.4 1.6 %collective-permute-start = (bf16[33,32,512]{2,1,0:T(8,128)(2,1)}, bf16[33,32,512]{2,1,0:T(8,128)(2,1)}, u32[]{:S(2)}, u32[]{:S(2)}) collective-permute-start(bf16[33,32,512]{2,1,0:T(8,128)(2,1)} %pad_maximum_fusion), channel_id=1, source_target_pairs={{4,8},{8,4},{12,16},{16,12},{20,24},{24,20},{5,9},{9,5},{13,17},{1... | collective-permute-start | bytes 3244040 | tf_op jit(solution)/shard_map/ppermute | solution.py:251
  7.2 3.3 %constant_dynamic-slice_fusion.1 = (bf16[32,8,1,512]{3,2,1,0:T(2,128)(2,1)S(1)}, bf16[32,8,1,512]{3,2,1,0:T(2,128)(2,1)S(1)}) fusion(bf16[32,8,32,512]{3,2,1,0:T(8,128)(2,1)} %param.14, s32[]{:T(128)S(6)} %select_n.128, s32[]{:T(128)S(6)} %select_n.127), kind=kLoop, calls=%fused_computation.110 | loop fusion | bytes 1048584 | tf_op jit(solution)/shard_map/jit(dynamic_index_in_dim)/dynamic_slice | solution.py:258
  11.0 2.5 %collective-permute-start.2 = (bf16[33,8,512]{2,1,0:T(8,128)(2,1)S(1)}, bf16[33,8,512]{2,1,0:T(8,128)(2,1)S(1)}, u32[]{:S(2)}, u32[]{:S(2)}) collective-permute-start(bf16[33,8,512]{2,1,0:T(8,128)(2,1)S(1)} %pad_maximum_fusion.2), channel_id=1, source_target_pairs={{0,1},{1,0},{2,3},{3,2},{4,5},{5,4},{6,7},{7,6},{8,9},{9,8},{10,11... | collective-permute-start | bytes 811016 | tf_op jit(solution)/shard_map/ppermute | solution.py:253
  13.6 1.4 collective-permute-start.3
  16.1 1.0 fusion.6.refs_9_.refs_12_
  17.8 0.6 pad_add_fusion.refs_0_
  18.8 0.3 copy.43
  19.4 1.4 concatenate.38
  20.9 0.9 pad.53.refs_10_.refs_13_
  21.9 0.7 pad.56.refs_15_.refs_18_
  22.7 0.6 pad.55.refs_14_.refs_17_
  23.4 0.6 pad.54.refs_13_.refs_16_
  23.9 0.8 pad.44.refs_2_
  24.7 1.2 add_convert_fusion.refs_8_.refs_11_
  25.9 0.8 broadcast_in_dim.130.refs_12_.refs_15_
  26.7 22.9 %first_step.1 = (bf16[32,256,512]{2,1,0:T(8,128)(2,1)}, bf16[33,32,512]{2,1,0:T(8,128)(2,1)}, bf16[33,32,512]{2,1,0:T(8,128)(2,1)}, bf16[33,8,512]{2,1,0:T(8,128...) custom-call(s32[2]{0:T(128)} %pad_add_fusion.refs_0_, ...), custom_call_target="tpu_custom_call" | custom-call | tf_op jit(solution)/shard_map/first_step/pallas_call | solution.py:209
  49.6 0.7 collective-permute-start.4
  50.3 3.8 %collective-permute-start.5 = (bf16[33,32,512]{2,1,0:T(8,128)(2,1)}, bf16[33,32,512]{2,1,0:T(8,128)(2,1)S(1)}, u32[]{:S(2)}, u32[]{:S(2)}) collective-permute-start(bf16[33,32,512]{2,1,0:T(8,128)(2,1)} %get-tuple-element.31), channel_id=1, source_target_pairs={{0,4},{4,0},{8,12},{12,8},{16,20},{20,16},{24,28},{28,24},{1,5},{5... | collective-permute-start | bytes 3244040 | tf_op jit(solution)/shard_map/ppermute | solution.py:252
  54.1 3.7 %collective-permute-start.6 = (bf16[33,8,512]{2,1,0:T(8,128)(2,1)}, bf16[33,8,512]{2,1,0:T(8,128)(2,1)S(1)}, u32[]{:S(2)}, u32[]{:S(2)}) collective-permute-start(bf16[33,8,512]{2,1,0:T(8,128)(2,1)} %get-tuple-element.32), channel_id=1, source_target_pairs={{0,1},{1,0},{2,3},{3,2},{4,5},{5,4},{6,7},{7,6},{8,9},{9,8},{10,11... | collective-permute-start | bytes 811016 | tf_op jit(solution)/shard_map/ppermute | solution.py:253
  57.8 0.7 collective-permute-start.7
  58.5 14.7 %all_to_all.31 = f32[32,1,128]{2,1,0:T(1,128)} all-to-all(f32[32,1,128]{2,1,0:T(1,128)} %bitcast.108), channel_id=1, replica_groups=mesh['gy'=8,'gx'=4] {'gy','gx'}, dimensions={0} | all-to-all | bytes 32768 | tf_op jit(solution)/shard_map/all_to_all | solution.py:336
  73.3 0.6 copy-done.9
  74.0 0.4 copy-done.4
  74.4 0.3 copy-done.5
  74.8 23.4 %mid_step.1 = (bf16[32,256,512]{2,1,0:T(8,128)(2,1)}, bf16[33,32,512]{2,1,0:T(8,128)(2,1)}, bf16[33,32,512]{2,1,0:T(8,128)(2,1)}, bf16[33,8,512]{2,1,0:T(8,128)(...) custom-call(s32[2]{0:T(128)} %pad_add_fusion.refs_0_, ...), custom_call_target="tpu_custom_call" | custom-call | tf_op jit(solution)/shard_map/mid_step/pallas_call | solution.py:209
  98.1 0.7 collective-permute-start.8
  98.9 1.9 %collective-permute-start.9 = (bf16[33,32,512]{2,1,0:T(8,128)(2,1)}, bf16[33,32,512]{2,1,0:T(8,128)(2,1)S(1)}, u32[]{:S(2)}, u32[]{:S(2)}) collective-permute-start(bf16[33,32,512]{2,1,0:T(8,128)(2,1)} %get-tuple-element.40), channel_id=1, source_target_pairs={{0,4},{4,0},{8,12},{12,8},{16,20},{20,16},{24,28},{28,24},{1,5},{5... | collective-permute-start | bytes 3244040 | tf_op jit(solution)/shard_map/ppermute | solution.py:252
  100.8 0.6 collective-permute-start.10
  101.4 0.7 collective-permute-start.11
  102.1 13.9 %all_to_all.32 = f32[32,1,128]{2,1,0:T(1,128)} all-to-all(f32[32,1,128]{2,1,0:T(1,128)} %bitcast.106), channel_id=1, replica_groups=mesh['gy'=8,'gx'=4] {'gy','gx'}, dimensions={0} | all-to-all | bytes 32768 | tf_op jit(solution)/shard_map/all_to_all | solution.py:336
  116.1 0.7 copy-done.7
  116.8 0.4 copy-done.2
  117.2 0.4 copy-done.3
  117.6 18.1 %last_step.1 = (f32[256,128]{1,0:T(8,128)}, f32[256,128]{1,0:T(8,128)}, f32[256,128]{1,0:T(8,128)}, f32[32,128]{1,0:T(8,128)}) custom-call(s32[2]{0:T(128)} %pad_add_fusion.refs_0_, f32[32]{0:T(128)} %refs_1_.5, f32[32,128]{1,0:T(8,128)} %bitcast.105, f32[256,128]{1,0:T(8,128)} %get-tuple-element.35.refs_3_, f32[128,128]{1,0:T(8,128)} %get-tuple-element.36.refs_4_, ...), custom_call_target="tpu_custom_call" | custom-call | tf_op jit(solution)/shard_map/last_step/pallas_call | solution.py:209
  135.8 3.7 %all-to-all-start.2 = ((f32[32,1,128]{2,1,0:T(1,128)}), f32[32,1,128]{2,1,0:T(1,128)S(1)}, u32[]{:S(2)}, u32[]{:S(2)}) async-start(f32[32,1,128]{2,1,0:T(1,128)} %bitcast.107), calls=%async_computation.2 | async-start | bytes 32768 | tf_op jit(solution)/shard_map/all_to_all | solution.py:336
  139.5 0.7 reduce_max.28
  140.1 0.7 reduce_max.29
  140.8 1.0 slice.31
  141.8 0.8 copy.50
  142.6 4.1 %all-to-all-done.2 = f32[32,1,128]{2,1,0:T(1,128)S(1)} async-done(((f32[32,1,128]{2,1,0:T(1,128)}), f32[32,1,128]{2,1,0:T(1,128)S(1)}, u32[]{:S(2)}, u32[]{:S(2)}) %all-to-all-start.2) | async-done | bytes 16416 | tf_op jit(solution)/shard_map/all_to_all | solution.py:336
  146.7 0.7 reduce_max.27
  148.1 1.1 slice_add_fusion
  149.2 0.8 copy.49
  149.9 2.6 %pad_maximum_fusion.4 = f32[3]{0:T(128)} fusion(f32[1]{0:T(128)} %bitcast.47, f32[1]{0:T(128)} %bitcast.46, f32[1]{0:T(128)} %bitcast.45), kind=kLoop, calls=%fused_computation.128 | loop fusion | flops 6 | bytes 24 | tf_op jit(solution)/shard_map/stack | solution.py:337
  (104 shorter events, 3.6 us)
Async XLA Ops:
  0.7 1.8 %copy-start.1 = (f32[32,8,32]{2,1,0:T(8,128)S(1)}, f32[32,8,32]{2,1,0:T(8,128)}, u32[]{:S(2)}) copy-start(f32[32,8,32]{2,1,0:T(8,128)} %param.9) | copy-start | bytes 98308
  3.8 22.1 %collective-permute-start.1 = (bf16[33,32,512]{2,1,0:T(8,128)(2,1)}, bf16[33,32,512]{2,1,0:T(8,128)(2,1)}, u32[]{:S(2)}, u32[]{:S(2)}) collective-permute-start(bf16[33,32,512]{2,1,0:T(8,128)(2,1)} %pad_maximum_fusion.1), channel_id=1, source_target_pairs={{0,4},{4,0},{8,12},{12,8},{16,20},{20,16},{24,28},{28,24},{1,5},{5... | collective-permute-start | bytes 3244040 | tf_op jit(solution)/shard_map/ppermute | solution.py:252
  5.4 20.5 %collective-permute-start = (bf16[33,32,512]{2,1,0:T(8,128)(2,1)}, bf16[33,32,512]{2,1,0:T(8,128)(2,1)}, u32[]{:S(2)}, u32[]{:S(2)}) collective-permute-start(bf16[33,32,512]{2,1,0:T(8,128)(2,1)} %pad_maximum_fusion), channel_id=1, source_target_pairs={{4,8},{8,4},{12,16},{16,12},{20,24},{24,20},{5,9},{9,5},{13,17},{1... | collective-permute-start | bytes 3244040 | tf_op jit(solution)/shard_map/ppermute | solution.py:251
  10.8 4.2 %copy-start.15 = (s32[4,8,32]{2,1,0:T(8,128)S(1)}, s32[4,8,32]{2,1,0:T(8,128)}, u32[]{:S(2)}) copy-start(s32[4,8,32]{2,1,0:T(8,128)} %param.17) | copy-start | bytes 12292
  10.8 4.7 %copy-start.16 = (f32[4,512]{1,0:T(4,128)S(1)}, f32[4,512]{1,0:T(4,128)}, u32[]{:S(2)}) copy-start(f32[4,512]{1,0:T(4,128)} %param.12) | copy-start | bytes 24580
  11.0 5.0 %copy-start.17 = (f32[32]{0:T(128)S(1)}, f32[32]{0:T(128)}, u32[]{:S(2)}) copy-start(f32[32]{0:T(128)} %refs_1_.5) | copy-start | bytes 388
  11.0 5.0 %copy-start.18 = (f32[4]{0:T(128)S(1)}, f32[4]{0:T(128)}, u32[]{:S(2)}) copy-start(f32[4]{0:T(128)} %param.13) | copy-start | bytes 52
  11.0 6.3 %copy-start.6 = (f32[4,32,8,32]{3,2,1,0:T(8,128)S(1)}, f32[4,32,8,32]{3,2,1,0:T(8,128)}, u32[]{:S(2)}) copy-start(f32[4,32,8,32]{3,2,1,0:T(8,128)} %param.11) | copy-start | bytes 393220
  11.0 14.9 %collective-permute-start.2 = (bf16[33,8,512]{2,1,0:T(8,128)(2,1)S(1)}, bf16[33,8,512]{2,1,0:T(8,128)(2,1)S(1)}, u32[]{:S(2)}, u32[]{:S(2)}) collective-permute-start(bf16[33,8,512]{2,1,0:T(8,128)(2,1)S(1)} %pad_maximum_fusion.2), channel_id=1, source_target_pairs={{0,1},{1,0},{2,3},{3,2},{4,5},{5,4},{6,7},{7,6},{8,9},{9,8},{10,11... | collective-permute-start | bytes 811016 | tf_op jit(solution)/shard_map/ppermute | solution.py:253
  13.6 12.3 %collective-permute-start.3 = (bf16[33,8,512]{2,1,0:T(8,128)(2,1)S(1)}, bf16[33,8,512]{2,1,0:T(8,128)(2,1)}, u32[]{:S(2)}, u32[]{:S(2)}) collective-permute-start(bf16[33,8,512]{2,1,0:T(8,128)(2,1)S(1)} %pad_maximum_fusion.3), channel_id=1, source_target_pairs={{1,2},{2,1},{5,6},{6,5},{9,10},{10,9},{13,14},{14,13},{17,18},{18,... | collective-permute-start | bytes 811016 | tf_op jit(solution)/shard_map/ppermute | solution.py:254
  17.6 1.6 %copy-start = (bf16[4,96,512]{2,1,0:T(8,128)(2,1)}, bf16[4,96,512]{2,1,0:T(8,128)(2,1)S(1)}, u32[]{:S(2)}) copy-start(bf16[4,96,512]{2,1,0:T(8,128)(2,1)S(1)} %multiply_dynamic-update-slice_fusion.2.refs_11_.refs_14_) | copy-start | bytes 1179652
  20.9 0.9 copy-start.14
  20.9 2.5 %copy-start.19 = (f32[32]{0:T(128)S(1)}, f32[32]{0:T(128)}, u32[]{:S(2)}) copy-start(f32[32]{0:T(128)} %param.16) | copy-start | bytes 388
  25.9 0.8 copy-start.11
  49.6 23.6 %collective-permute-start.4 = (bf16[33,32,512]{2,1,0:T(8,128)(2,1)}, bf16[33,32,512]{2,1,0:T(8,128)(2,1)S(1)}, u32[]{:S(2)}, u32[]{:S(2)}) collective-permute-start(bf16[33,32,512]{2,1,0:T(8,128)(2,1)} %get-tuple-element.30), channel_id=1, source_target_pairs={{4,8},{8,4},{12,16},{16,12},{20,24},{24,20},{5,9},{9,5},{13,17},{1... | collective-permute-start | bytes 3244040 | tf_op jit(solution)/shard_map/ppermute | solution.py:251
  50.3 22.9 %collective-permute-start.5 = (bf16[33,32,512]{2,1,0:T(8,128)(2,1)}, bf16[33,32,512]{2,1,0:T(8,128)(2,1)S(1)}, u32[]{:S(2)}, u32[]{:S(2)}) collective-permute-start(bf16[33,32,512]{2,1,0:T(8,128)(2,1)} %get-tuple-element.31), channel_id=1, source_target_pairs={{0,4},{4,0},{8,12},{12,8},{16,20},{20,16},{24,28},{28,24},{1,5},{5... | collective-permute-start | bytes 3244040 | tf_op jit(solution)/shard_map/ppermute | solution.py:252
  54.1 19.1 %collective-permute-start.6 = (bf16[33,8,512]{2,1,0:T(8,128)(2,1)}, bf16[33,8,512]{2,1,0:T(8,128)(2,1)S(1)}, u32[]{:S(2)}, u32[]{:S(2)}) collective-permute-start(bf16[33,8,512]{2,1,0:T(8,128)(2,1)} %get-tuple-element.32), channel_id=1, source_target_pairs={{0,1},{1,0},{2,3},{3,2},{4,5},{5,4},{6,7},{7,6},{8,9},{9,8},{10,11... | collective-permute-start | bytes 811016 | tf_op jit(solution)/shard_map/ppermute | solution.py:253
  57.8 15.4 %collective-permute-start.7 = (bf16[33,8,512]{2,1,0:T(8,128)(2,1)}, bf16[33,8,512]{2,1,0:T(8,128)(2,1)S(1)}, u32[]{:S(2)}, u32[]{:S(2)}) collective-permute-start(bf16[33,8,512]{2,1,0:T(8,128)(2,1)} %get-tuple-element.33), channel_id=1, source_target_pairs={{1,2},{2,1},{5,6},{6,5},{9,10},{10,9},{13,14},{14,13},{17,18},{18,... | collective-permute-start | bytes 811016 | tf_op jit(solution)/shard_map/ppermute | solution.py:254
  73.2 0.7 copy-start.9
  73.2 0.8 copy-start.10
  73.2 1.2 copy-start.4
  73.3 1.5 copy-start.5
  98.1 17.9 %collective-permute-start.8 = (bf16[33,32,512]{2,1,0:T(8,128)(2,1)}, bf16[33,32,512]{2,1,0:T(8,128)(2,1)S(1)}, u32[]{:S(2)}, u32[]{:S(2)}) collective-permute-start(bf16[33,32,512]{2,1,0:T(8,128)(2,1)} %get-tuple-element.39), channel_id=1, source_target_pairs={{4,8},{8,4},{12,16},{16,12},{20,24},{24,20},{5,9},{9,5},{13,17},{1... | collective-permute-start | bytes 3244040 | tf_op jit(solution)/shard_map/ppermute | solution.py:251
  98.9 17.2 %collective-permute-start.9 = (bf16[33,32,512]{2,1,0:T(8,128)(2,1)}, bf16[33,32,512]{2,1,0:T(8,128)(2,1)S(1)}, u32[]{:S(2)}, u32[]{:S(2)}) collective-permute-start(bf16[33,32,512]{2,1,0:T(8,128)(2,1)} %get-tuple-element.40), channel_id=1, source_target_pairs={{0,4},{4,0},{8,12},{12,8},{16,20},{20,16},{24,28},{28,24},{1,5},{5... | collective-permute-start | bytes 3244040 | tf_op jit(solution)/shard_map/ppermute | solution.py:252
  100.8 15.2 %collective-permute-start.10 = (bf16[33,8,512]{2,1,0:T(8,128)(2,1)}, bf16[33,8,512]{2,1,0:T(8,128)(2,1)S(1)}, u32[]{:S(2)}, u32[]{:S(2)}) collective-permute-start(bf16[33,8,512]{2,1,0:T(8,128)(2,1)} %get-tuple-element.41), channel_id=1, source_target_pairs={{0,1},{1,0},{2,3},{3,2},{4,5},{5,4},{6,7},{7,6},{8,9},{9,8},{10,11... | collective-permute-start | bytes 811016 | tf_op jit(solution)/shard_map/ppermute | solution.py:253
  101.4 14.6 %collective-permute-start.11 = (bf16[33,8,512]{2,1,0:T(8,128)(2,1)}, bf16[33,8,512]{2,1,0:T(8,128)(2,1)S(1)}, u32[]{:S(2)}, u32[]{:S(2)}) collective-permute-start(bf16[33,8,512]{2,1,0:T(8,128)(2,1)} %get-tuple-element.42), channel_id=1, source_target_pairs={{1,2},{2,1},{5,6},{6,5},{9,10},{10,9},{13,14},{14,13},{17,18},{18,... | collective-permute-start | bytes 811016 | tf_op jit(solution)/shard_map/ppermute | solution.py:254
  116.0 0.7 copy-start.7
  116.0 0.8 copy-start.8
  116.1 1.2 copy-start.2
  116.1 1.6 %copy-start.3 = (bf16[33,32,512]{2,1,0:T(8,128)(2,1)}, bf16[33,32,512]{2,1,0:T(8,128)(2,1)S(1)}, u32[]{:S(2)}) copy-start(bf16[33,32,512]{2,1,0:T(8,128)(2,1)S(1)} %collective-permute-done.9.refs_8_) | copy-start | bytes 3244036
  117.6 21.8 %copy-start.12 = (f32[32,1,128]{2,1,0:T(1,128)S(1)}, f32[32,1,128]{2,1,0:T(1,128)}, u32[]{:S(2)}) copy-start(f32[32,1,128]{2,1,0:T(1,128)} %all_to_all.31) | copy-start | bytes 49156
  117.6 22.5 %copy-start.13 = (f32[32,1,128]{2,1,0:T(1,128)S(1)}, f32[32,1,128]{2,1,0:T(1,128)}, u32[]{:S(2)}) copy-start(f32[32,1,128]{2,1,0:T(1,128)} %all_to_all.32) | copy-start | bytes 49156
  135.8 10.9 %all-to-all-start.2 = ((f32[32,1,128]{2,1,0:T(1,128)}), f32[32,1,128]{2,1,0:T(1,128)S(1)}, u32[]{:S(2)}, u32[]{:S(2)}) async-start(f32[32,1,128]{2,1,0:T(1,128)} %bitcast.107), calls=%async_computation.2 | async-start | bytes 32768 | tf_op jit(solution)/shard_map/all_to_all | solution.py:336
where the time goes:
time: 153 us
  Pallas kernels  64.5 us (42%)
  blocking collectives  28.6 us (19%)
  starting transfers between devices  22.5 us (15%)
  local copies, waits for them, and re-layouts  19.1 us (12%)
  other arithmetic  11.7 us (8%)
  waiting for transfers between devices  4.09 us (3%)
  between operations  1.99 us (1%)
    pallas_call x3, Pallas kernels, run_step(): pl.pallas_call(functools.partial(step_kernel, dims, first, last), out_sha...  64.5 us
    all_to_all x2, blocking collectives, local(): peaks.append(lax.all_to_all(peak, ('gy', 'gx'), 0, 0, tiled=True))  28.6 us
    ppermute x3, starting transfers between devices, exchange(): lax.ppermute(pC, 'gx', near_x)  6.84 us
    ppermute x3, starting transfers between devices, exchange(): lax.ppermute(pA, 'gy', near_y)  6.2 us
    unnamed x45, local copies, waits for them, and re-layouts  4.81 us
    all_to_all x1, waiting for transfers between devices, local(): peaks.append(lax.all_to_all(peak, ('gy', 'gx'), 0, 0, tiled=True))  4.06 us
    all_to_all x1, starting transfers between devices, local(): peaks.append(lax.all_to_all(peak, ('gy', 'gx'), 0, 0, tiled=True))  3.67 us
    dynamic_slice x1, local copies, waits for them, and re-layouts, first_payload(): state = lax.dynamic_index_in_dim(prior_probs, index, axis, keepdims=False)  3.33 us
  transfers between devices with their start and end apart: 13, of which 1 were waited for; matrix products, arithmetic and copies ran while one was open for 12% of the time, Pallas kernels for 0%

commit v1 on v0

v1 whole, which is shorter than its diff:
```python
import functools
import math

import jax
import jax.numpy as jnp
from jax import lax
from jax.experimental import pallas as pl
from jax.experimental.pallas import tpu as pltpu
from jax.sharding import PartitionSpec as P

ITERS = 3
step_level = 0.2
gap_eps = 1e-06
LANES = 128
GROUP = 4
PARTS = 3
LEFT = (0, 0, 1, 0, 1, 2)
RIGHT = (0, 1, 0, 2, 1, 0)
F32 = jnp.float32
BF16 = jnp.bfloat16
LOG2E = 1.0 / math.log(2.0)
VMEM = pl.BlockSpec(memory_space=pltpu.VMEM)
SMEM = pl.BlockSpec(memory_space=pltpu.SMEM)
ANY = pl.BlockSpec(memory_space=pl.ANY)


def shape(dims, dtype=F32):
    return jax.ShapeDtypeStruct(dims, dtype)


def call(body, name, args, in_specs, out_shape, scratch=(), mib=8, out_specs=None):
    return pl.pallas_call(
        body,
        out_shape=out_shape,
        in_specs=in_specs,
        out_specs=out_specs or tuple(VMEM for _ in out_shape),
        scratch_shapes=list(scratch),
        compiler_params=pltpu.CompilerParams(vmem_limit_bytes=mib * 1024 * 1024),
        name=name,
    )(*args)


def kernel_parts(x, count):
    parts = []
    for _ in range(count):
        part = x.astype(BF16)
        parts.append(part)
        x = x - part.astype(F32)
    return parts


def dot(a, b):
    return jnp.dot(a, b, preferred_element_type=F32)


def iota(dims, axis):
    return lax.broadcasted_iota(jnp.int32, dims, axis)


def side_columns(x, lo):
    return jnp.concatenate([jnp.zeros((lo, x.shape[1]), F32), x], axis=0).T


def plane(ref, at, values):
    hi, mid = kernel_parts(values, 2)
    width = ref.shape[-1]
    ref[at, :, 0:LANES] = hi
    ref[at, :, LANES : 2 * LANES] = mid
    ref[at, :, 2 * LANES :] = jnp.zeros((values.shape[0], width - 2 * LANES), BF16)


def rows_kernel(dims, parity, mean, prior, pB, pA, sems):
    J, TR, TC, R, ND = dims
    lo = LANES - J
    py = parity[0]
    row_b, row_a = py * (TR - 1), (1 - py) * (TR - 1)
    copies = []
    for n, (ref, row) in enumerate(((pB, row_b), (pA, row_a))):
        copy = pltpu.make_async_copy(prior.at[:, row], ref.at[pl.ds(0, J)], sems.at[n])
        copy.start()
        copies.append(copy)
    north = side_columns(mean[:, 0, :], lo)
    south = side_columns(mean[:, TR - 1, :], lo)
    plane(pB, J, jnp.where(py == 1, south, north))
    plane(pA, J, jnp.where(py == 1, north, south))
    for copy in copies:
        copy.wait()


def prep_kernel(dims, K, *refs):
    J, TR, TC, R, ND = dims
    M = TR * TC
    lo = LANES - J
    (parity, scale_s, spill, rates, mean, shares, chars, draws, links) = refs[:9]
    (Wl, Wc, T4, dsel, cnt, rate, ispill, table, logobs) = refs[9:18]
    taste, a_s = refs[18:]
    py, px = parity[0], parity[1]

    columns = links[...].astype(F32).reshape(4 * TR, TC)
    columns = jnp.concatenate([columns, jnp.zeros((LANES - 4 * TR, TC), F32)], axis=0).T
    for d in range(4):
        for i in range(TR):
            at = d * TR + i
            a_s[d, i * TC : (i + 1) * TC, :] = jnp.broadcast_to(columns[:, at : at + 1], (TC, LANES))
    count = jnp.maximum(a_s[0] + a_s[1] + a_s[2] + a_s[3], 1.0)
    cnt[...] = count

    me = iota((M, LANES), 0)
    lane = iota((M, LANES), 1)
    r, c = me // TC, me % TC
    for b in range(M // LANES):
        other = lane + b * LANES
        w = jnp.where(other == me - TC, a_s[0], 0.0)
        w = w + jnp.where(other == me + TC, a_s[1], 0.0)
        w = w + jnp.where((other == me - 1) & (c > 0), a_s[2], 0.0)
        w = w + jnp.where((other == me + 1) & (c < TC - 1), a_s[3], 0.0)
        Wl[:, b * LANES : (b + 1) * LANES] = w.astype(BF16)
    north = jnp.where(r == 0, a_s[0], 0.0)
    south = jnp.where(r == TR - 1, a_s[1], 0.0)
    west = jnp.where(c == 0, a_s[2], 0.0)
    east = jnp.where(c == TC - 1, a_s[3], 0.0)
    far_row = jnp.where(py == 1, south, north)
    near_row = jnp.where(py == 1, north, south)
    near_col = jnp.where(px == 1, west, east)
    far_col = jnp.where(px == 1, east, west)
    Wc[...] = (
        jnp.where(lane == c, far_row, 0.0)
        + jnp.where(lane == TC + c, near_row, 0.0)
        + jnp.where(lane == 2 * TC + r, near_col, 0.0)
        + jnp.where(lane == 2 * TC + TR + r, far_col, 0.0)
    ).astype(BF16)
    inverse = 1.0 / spill[...]
    left = jnp.zeros((1, lo), F32)
    rate[...] = jnp.concatenate([left, rates[...]], axis=1)
    ispill[...] = jnp.concatenate([left, inverse], axis=1)
    per_rate = jnp.concatenate([inverse * scale_s[k] for k in range(K)], axis=1)
    for i in range(TR):
        at = slice(i * TC, (i + 1) * TC)
        table[at] = side_columns(mean[:, i, :], lo)
        logobs[at] = side_columns(jnp.log(shares[:, i, :]), lo)
        block = jnp.concatenate([chars[k, :, i, :] for k in range(K)], axis=0).T
        taste[at] = block * per_rate
    parts = kernel_parts(taste[...] * count, PARTS)
    width = GROUP * K
    src = iota((LANES, LANES), 0)
    dst = iota((LANES, LANES), 1)
    term, inner = dst // width, dst % width
    for g in range(J // GROUP):
        wanted = (inner // GROUP) * J + g * GROUP + inner % GROUP
        hit = (src == wanted) & (term < len(LEFT))
        total = jnp.zeros((M, LANES), F32)
        for p in range(PARTS):
            which = functools.reduce(jnp.logical_or, [term == t for t, l in enumerate(LEFT) if l == p])
            total = total + dot(parts[p], jnp.where(hit & which, 1.0, 0.0).astype(BF16))
        T4[g] = total.astype(BF16)

    d_parts = kernel_parts(draws[...], PARTS)
    held = jnp.concatenate([p.astype(F32) for p in d_parts], axis=0)
    held = jnp.concatenate([held, jnp.zeros((LANES - PARTS * K, R), F32)], axis=0).astype(BF16)
    src = iota((LANES, LANES), 1)
    dst = iota((LANES, LANES), 0)
    term, inner = dst // width, dst % width
    for q in range(GROUP):
        hit = jnp.zeros((LANES, LANES), jnp.bool_)
        for t, p in enumerate(RIGHT):
            hit = hit | ((term == t) & (src == p * K + inner // GROUP))
        hit = hit & (inner % GROUP == q)
        dsel[q] = dot(jnp.where(hit, 1.0, 0.0).astype(BF16), held).astype(BF16)


def columns_kernel(dims, parity, mean, state, pC, pD):
    J, TR, TC, R, ND = dims
    M = TR * TC
    lo = LANES - J
    px = parity[1]
    line = iota((2 * TR, M), 0)
    col = jnp.where(line < TR, (1 - px) * (TC - 1), px * (TC - 1))
    pick = jnp.where(iota((2 * TR, M), 1) == (line % TR) * TC + col, 1.0, 0.0).astype(BF16)

    def body(g, carry):
        for q in range(GROUP):
            j = g * GROUP + q
            found = dot(pick, state[j]).astype(BF16)
            pC[j] = found[:TR]
            pD[j] = found[TR:]
        return carry

    lax.fori_loop(0, J // GROUP, body, 0)
    west, east = [], []
    for i in range(TR):
        block = side_columns(mean[:, i, :], lo)
        west.append(block[0:1])
        east.append(block[TC - 1 : TC])
    west = jnp.concatenate(west, axis=0)
    east = jnp.concatenate(east, axis=0)
    plane(pC, J, jnp.where(px == 0, east, west))
    plane(pD, J, jnp.where(px == 0, west, east))


def step_kernel(dims, first, last, *refs):
    J, TR, TC, R, ND = dims
    M = TR * TC
    lo = LANES - J
    refs = list(refs)
    parity = refs.pop(0)
    spill = refs.pop(0)
    if not first:
        mall, res_in, mh_in = refs[:3]
        refs = refs[3:]
    mean_in, state, hB, hA, hC, hD, Wl, Wc, T4, dsel, cnt, rate, ispill, logobs = refs[:14]
    refs = refs[14:]
    if last:
        mean_out, res_out, log_out, mloc = refs[:4]
        refs = refs[4:]
    else:
        state_out, pB, pA, pC, pD, mean_out, res_out, mh_out, mloc = refs[:9]
        refs = refs[9:]
    E, den, Wcb, W4b, S_ref, sc_ref = refs[:6]
    if not last:
        colf = refs[6]

    rim = []
    for h in (hB, hA, hC, hD):
        rim.append(h[J, :, 0:LANES].astype(F32) + h[J, :, LANES : 2 * LANES].astype(F32))
    rim.append(jnp.zeros((LANES - 2 * (TR + TC), LANES), F32))
    rim = jnp.concatenate(rim, axis=0)
    if first:
        mean = mean_in[...]
        mh = rim
    else:
        step = step_level / (jnp.max(mall[...]) + gap_eps)
        mean = mean_in[...] + step * res_in[...]
        mh = mh_in[...] + step * rim
    mean_out[...] = mean
    if not last:
        mh_out[...] = mh
    acc = jnp.zeros((M, LANES), F32)
    for part in kernel_parts(mean, 3):
        acc = acc + dot(Wl[...], part)
    for part in kernel_parts(mh, 3):
        acc = acc + dot(Wc[...], part)
    scaled = (mean * cnt[...] + rate[...] * acc) * ispill[...]
    b_hi, b_mid = kernel_parts(scaled, 2)
    Wcb[...] = Wc[...] + b_hi
    for g in range(J // GROUP):
        W4b[g] = T4[g] + b_mid
    sc_ref[...] = LOG2E / cnt[...]
    den[...] = jnp.ones_like(den)

    row_id = iota((J, R), 0)
    zeros_mid = jnp.zeros((lo - 2 * (TR + TC), R), BF16)

    def pass_one(g, carry):
        for q in range(GROUP):
            j = g * GROUP + q
            onehot = jnp.where(row_id == j, 1.0, 0.0).astype(BF16)
            cd = jnp.concatenate([hC[j].astype(F32), hD[j].astype(F32)], axis=0).astype(BF16)
            rhs = jnp.concatenate([hB[j], hA[j], cd, zeros_mid, onehot, dsel[q, :lo, :], onehot], axis=0)
            lhs = jnp.concatenate([Wcb[...], W4b[g]], axis=1)
            total = dot(Wl[...], state[j]) + dot(lhs, rhs)
            factor = sc_ref[...] * spill[j]
            factor = jnp.concatenate([factor] * (R // LANES), axis=1)
            e = jnp.exp2(total * factor)
            E[j] = e
            den[...] += e
        return carry

    lax.fori_loop(0, J // GROUP, pass_one, 0)

    lane = iota((TC, LANES), 1)

    def chunk(row, carry):
        rows = pl.ds(pl.multiple_of(row * TC, TC), TC)
        inverse = 1.0 / den[rows, :]
        sums = jnp.zeros((TC, LANES), F32)
        for j in range(J):
            prob = E[j, rows, :] * inverse
            if not last:
                state_out[j, rows, :] = prob.astype(BF16)
                colf[0, j, pl.ds(row, 1), :] = prob[0:1]
                colf[1, j, pl.ds(row, 1), :] = prob[TC - 1 : TC]
            part = prob[:, 0:LANES]
            for b in range(1, R // LANES):
                part = part + prob[:, b * LANES : (b + 1) * LANES]
            sums = jnp.where(lane == lo + j, jnp.sum(part, axis=1, keepdims=True), sums)
        S_ref[rows, :] = sums
        return carry

    lax.fori_loop(0, TR, chunk, 0)

    log_pred = jnp.log(S_ref[...] * (1.0 / R))
    res = jnp.where(iota((M, LANES), 1) >= lo, logobs[...] - log_pred, 0.0)
    res_out[...] = res
    mloc[...] = jnp.broadcast_to(jnp.max(jnp.abs(res)), (ND, LANES))
    if last:
        log_out[...] = log_pred
        return

    py = parity[0]
    px = parity[1]
    for ref, start in ((pB, py * (M - TC)), (pA, (1 - py) * (M - TC))):
        rows = pl.ds(pl.multiple_of(start, TC), TC)
        plane(ref, J, res_out[rows, :])

        def copy_rows(j, carry, ref=ref, rows=rows):
            ref[j] = state_out[j, rows, :]
            return carry

        lax.fori_loop(0, J, copy_rows, 0, unroll=4)
    west = res_out[pl.ds(0, TR, stride=TC), :]
    east = res_out[pl.ds(TC - 1, TR, stride=TC), :]
    plane(pC, J, jnp.where(px == 0, east, west))
    plane(pD, J, jnp.where(px == 0, west, east))

    def copy_cols(j, carry):
        pC[j] = colf[1 - px, j].astype(BF16)
        pD[j] = colf[px, j].astype(BF16)
        return carry

    lax.fori_loop(0, J, copy_cols, 0, unroll=4)


def layout_kernel(dims, mean, res, log_pred, mean_t, res_t, log_t):
    J, TR, TC, R, ND = dims
    lo = LANES - J
    for ref, out in ((mean, mean_t), (res, res_t), (log_pred, log_t)):
        for i in range(TR):
            out[:, i, :] = ref[i * TC : (i + 1) * TC, :].T[lo:]


def final_kernel(*refs):
    peaks = refs[:ITERS]
    mean_t, res_t, final, worst = refs[ITERS:]
    for n, peak in enumerate(peaks):
        worst[n] = jnp.max(peak[...])
    step = step_level / (jnp.max(peaks[-1][...]) + gap_eps)
    final[...] = mean_t[...] + step * res_t[...]


def pair_perms(size):
    near = [(i, i ^ 1) for i in range(size) if (i ^ 1) < size]
    far = [(i, i + 1 if i % 2 else i - 1) for i in range(size)]
    far = [(i, k) for i, k in far if 0 <= k < size]
    return near, far


def local(
    mean_util,
    observed_shares,
    characteristics,
    taste_draws,
    taste_scale,
    prior_probs,
    spill_rate,
    utility_rate,
    adjacency,
):
    J, TR, TC = mean_util.shape
    K, R = taste_draws.shape
    M = TR * TC
    lo = LANES - J
    ny, nx = lax.axis_size("gy"), lax.axis_size("gx")
    dims = (J, TR, TC, R, ny * nx)
    py = lax.axis_index("gy") % 2
    px = lax.axis_index("gx") % 2
    parity = jnp.stack([py, px]).astype(jnp.int32)
    near_y, far_y = pair_perms(ny)
    near_x, far_x = pair_perms(nx)

    table = shape((M, LANES))
    row = shape((J + 1, TC, R), BF16)
    col = shape((J + 1, TR, R), BF16)
    peak_shape = shape((ny * nx, LANES))
    cube = shape((J, TR, TC))

    pB, pA = call(
        functools.partial(rows_kernel, dims),
        "rows",
        (parity, mean_util, pltpu.with_memory_space_constraint(prior_probs, pltpu.HBM)),
        [SMEM, VMEM, ANY],
        (row, row),
        [pltpu.SemaphoreType.DMA((2,))],
    )

    def exchange(pB, pA, pC, pD):
        return (
            lax.ppermute(pB, "gy", far_y),
            lax.ppermute(pA, "gy", near_y),
            lax.ppermute(pC, "gx", near_x),
            lax.ppermute(pD, "gx", far_x),
        )

    pC, pD = call(
        functools.partial(columns_kernel, dims),
        "columns",
        (parity, mean_util, prior_probs.reshape(J, M, R)),
        [SMEM, VMEM, VMEM],
        (col, col),
    )
    halos = exchange(pB, pA, pC, pD)

    Wl, Wc, T4, dsel, cnt, rate, ispill, mean, logobs = call(
        functools.partial(prep_kernel, dims, K),
        "prep",
        (
            parity,
            taste_scale,
            spill_rate.reshape(1, J),
            utility_rate.reshape(1, J),
            mean_util,
            observed_shares,
            characteristics,
            taste_draws,
            adjacency,
        ),
        [SMEM, SMEM] + [VMEM] * 7,
        (
            shape((M, M), BF16),
            shape((M, LANES), BF16),
            shape((J // GROUP, M, LANES), BF16),
            shape((GROUP, LANES, R), BF16),
            table,
            shape((1, LANES)),
            shape((1, LANES)),
            table,
            table,
        ),
        [pltpu.VMEM((M, LANES), F32), pltpu.VMEM((4, M, LANES), F32)],
    )

    state = prior_probs.reshape(J, M, R)
    peaks = []
    res = rim = None
    for iteration in range(ITERS):
        first, last = iteration == 0, iteration + 1 == ITERS
        moving = () if first else (peaks[-1], res, rim)
        args = (parity, spill_rate) + moving + (mean, state) + halos
        args = args + (Wl, Wc, T4, dsel, cnt, rate, ispill, logobs)
        if last:
            outs = (table, table, table, peak_shape)
        else:
            outs = (shape((J, M, R), BF16), row, row, col, col, table, table, shape((LANES, LANES)), peak_shape)
        scratch = [
            pltpu.VMEM((J, M, R), F32),
            pltpu.VMEM((M, R), F32),
            pltpu.VMEM((M, LANES), BF16),
            pltpu.VMEM((J // GROUP, M, LANES), BF16),
            pltpu.VMEM((M, LANES), F32),
            pltpu.VMEM((M, LANES), F32),
        ]
        if not last:
            scratch.append(pltpu.VMEM((2, J, TR, R), F32))
        out = call(
            functools.partial(step_kernel, dims, first, last),
            "step",
            args,
            [SMEM, SMEM] + [VMEM] * (len(args) - 2),
            outs,
            scratch,
            mib=23,
        )
        if last:
            mean, res, log_pred, peak = out
        else:
            state, pB, pA, pC, pD, mean, res, rim, peak = out
            halos = exchange(pB, pA, pC, pD)
        peaks.append(lax.all_to_all(peak, ("gy", "gx"), 0, 0, tiled=True))

    mean_t, res_t, log_t = call(
        functools.partial(layout_kernel, dims), "layout", (mean, res, log_pred), [VMEM] * 3, (cube, cube, cube)
    )
    final, worst = call(
        final_kernel,
        "final",
        tuple(peaks) + (mean_t, res_t),
        [VMEM] * (ITERS + 2),
        (cube, shape((ITERS,))),
        out_specs=(VMEM, SMEM),
    )
    return final, log_t, worst


def solution(mesh):
    placed = (
        P(None, "gy", "gx"),
        P(None, "gy", "gx"),
        P(None, None, "gy", "gx"),
        P(),
        P(),
        P(None, "gy", "gx", None),
        P(),
        P(),
        P(None, "gy", "gx"),
    )
    return jax.shard_map(
        local,
        mesh=mesh,
        in_specs=placed,
        out_specs=(P(None, "gy", "gx"), P(None, "gy", "gx"), P()),
        check_vma=False,
    )
```

time: 153 us -> 106 us (0.69)
  Pallas kernels: 64.5 us -> 39 us
  local copies, waits for them, and re-layouts: 19.1 us -> 0.95 us
  other arithmetic: 11.7 us -> 0.08 us
  waiting for transfers between devices: 4.09 us -> 11.1 us
  starting transfers between devices: 22.5 us -> 25.9 us
    pallas_call x3 -> x8, Pallas kernels: 64.5 us -> 39 us  [call(): pl.pallas_call(body, out_shape=out_shape, in_specs=in_specs, out_specs=ou...]
    ppermute x3, waiting for transfers between devices: 0.01 us -> 5.14 us  [exchange(): lax.ppermute(pC, 'gx', near_x)]
    dynamic_slice x7 -> x0, local copies, waits for them, and re-layouts: 3.88 us -> none  [the longest x1 3.33 us: first_payload(): state = lax.dynamic_index_in_dim(prior_probs, index, axis, keepdims=False)]
    unnamed x45 -> x20, local copies, waits for them, and re-layouts: 4.81 us -> 0.95 us
    pad x5 -> x0, local copies, waits for them, and re-layouts: 3.66 us -> none  [the longest x1 0.92 us: local(): T4 = jnp.pad(T4, ((0, 0), (0, 0), (0, LANES - T4.shape[2])))]
    ppermute x3, starting transfers between devices: 6.2 us -> 9.81 us  [exchange(): lax.ppermute(pA, 'gy', near_y)]
    another operation x1 -> x0, other arithmetic: 2.57 us -> none  [local(): worst = jnp.stack([jnp.max(p) for p in peaks])]
    convert_element_type x8 -> x0, other arithmetic: 2.42 us -> none  [the longest x1 1.18 us: local(): Wl = (jnp.where(other == me - TC, links[0], 0.0) + jnp.where(other == me...]
  transfers between devices with their start and end apart: 13 -> 13, of which waited for: 1 -> 2; matrix products, arithmetic and copies ran while one was open for 12% -> 0% of each run, Pallas kernels for 0% -> 6%
where the time goes in v1:
time: 106 us
  Pallas kernels  39 us (37%)
  blocking collectives  27.6 us (26%)
  starting transfers between devices  25.9 us (24%)
  waiting for transfers between devices  11.1 us (10%)
    pallas_call x8, Pallas kernels, call(): pl.pallas_call(body, out_shape=out_shape, in_specs=in_specs, out_specs=ou...  39 us
    all_to_all x2, blocking collectives, local(): peaks.append(lax.all_to_all(peak, ('gy', 'gx'), 0, 0, tiled=True))  27.6 us
    ppermute x3, starting transfers between devices, exchange(): lax.ppermute(pA, 'gy', near_y)  9.81 us
    ppermute x3, starting transfers between devices, exchange(): lax.ppermute(pC, 'gx', near_x)  8.92 us
    all_to_all x1, waiting for transfers between devices, local(): peaks.append(lax.all_to_all(peak, ('gy', 'gx'), 0, 0, tiled=True))  5.98 us
    ppermute x3, waiting for transfers between devices, exchange(): lax.ppermute(pC, 'gx', near_x)  5.14 us
    all_to_all x1, starting transfers between devices, local(): peaks.append(lax.all_to_all(peak, ('gy', 'gx'), 0, 0, tiled=True))  2.88 us
    ppermute x3, starting transfers between devices, exchange(): lax.ppermute(pB, 'gy', far_y)  2.32 us
  transfers between devices with their start and end apart: 13, of which 2 were waited for; matrix products, arithmetic and copies ran while one was open for 0% of the time, Pallas kernels for 6%

profile of v1, /device:TPU:0, one launch (start us, length us, event | category | flops | bytes accessed | tf_op | source)
XLA Modules:
  0.0 105.6 jit_solution(16161369155272686676)
XLA Ops:
  0.6 0.1 pad_add_fusion.refs_0_.parity
  0.7 0.9 copy-done.1
  1.6 2.3 %rows.1 = (bf16[33,32,512]{2,1,0:T(8,128)(2,1)S(1)}, bf16[33,32,512]{2,1,0:T(8,128)(2,1)S(1)}) custom-call(s32[2]{0:T(128)S(1)} %pad_add_fusion.refs_0_.parity, f32[32,8,32]{2,1,0:T(8,128)S(1)} %copy-done.1, bf16[32,8,32,512]{3,2,1,0:T(8,128)(2,1)} %prior.1), custom_call_target="tpu_custom_call" | custom-call | tf_op jit(solution)/shard_map/rows/pallas_call | solution.py:32
  4.0 0.9 collective-permute-start
  4.9 4.4 %collective-permute-start.1 = (bf16[33,32,512]{2,1,0:T(8,128)(2,1)S(1)}, bf16[33,32,512]{2,1,0:T(8,128)(2,1)S(1)}, u32[]{:S(2)}, u32[]{:S(2)}) collective-permute-start(bf16[33,32,512]{2,1,0:T(8,128)(2,1)S(1)} %get-tuple-element.45), channel_id=1, source_target_pairs={{0,4},{4,0},{8,12},{12,8},{16,20},{20,16},{24,28},{28,24},{1,5},{5... | collective-permute-start | bytes 3244040 | tf_op jit(solution)/shard_map/ppermute | solution.py:388
  9.3 0.0 copy-start.5
  9.3 0.0 copy-start.6
  9.3 0.0 copy-start.7
  9.3 0.0 copy-start.8
  9.3 0.0 copy-start.9
  9.3 2.7 %columns.1 = (bf16[33,8,512]{2,1,0:T(8,128)(2,1)S(1)}, bf16[33,8,512]{2,1,0:T(8,128)(2,1)S(1)}) custom-call(s32[2]{0:T(128)S(1)} %pad_add_fusion.refs_0_.parity, f32[32,8,32]{2,1,0:T(8,128)S(1)} %copy-done.1, bf16[32,256,512]{2,1,0:T(8,128)(2,1)S(1)} %bitcast.17), custom_call_target="tpu_custom_call" | custom-call | tf_op jit(solution)/shard_map/columns/pallas_call | solution.py:32
  12.1 1.6 %collective-permute-start.2 = (bf16[33,8,512]{2,1,0:T(8,128)(2,1)S(1)}, bf16[33,8,512]{2,1,0:T(8,128)(2,1)S(1)}, u32[]{:S(2)}, u32[]{:S(2)}) collective-permute-start(bf16[33,8,512]{2,1,0:T(8,128)(2,1)S(1)} %get-tuple-element.46), channel_id=1, source_target_pairs={{0,1},{1,0},{2,3},{3,2},{4,5},{5,4},{6,7},{7,6},{8,9},{9,8},{10,11... | collective-permute-start | bytes 811016 | tf_op jit(solution)/shard_map/ppermute | solution.py:389
  13.6 0.7 collective-permute-start.3
  14.3 0.0 copy-done.2
  14.3 0.0 copy-done.3
  14.3 0.0 copy-done.4
  14.3 0.0 copy-done.5
  14.3 0.0 copy-done.6
  14.4 2.0 %prep.1 = (bf16[256,256]{1,0:T(8,128)(2,1)S(1)}, bf16[256,128]{1,0:T(8,128)(2,1)S(1)}, bf16[8,256,128]{2,1,0:T(8,128)(2,1)S(1)}, bf16[4,128,512]{2,1,0:T(8,128)(...) custom-call(s32[2]{0:T(128)S(1)} %pad_add_fusion.refs_0_.parity, ...), custom_call_target="tpu_custom_call" | custom-call | tf_op jit(solution)/shard_map/prep/pallas_call | solution.py:32
  16.4 5.1 %collective-permute-done.2.refs_6_ = bf16[33,8,512]{2,1,0:T(8,128)(2,1)S(1)} collective-permute-done((bf16[33,8,512]{2,1,0:T(8,128)(2,1)S(1)}, bf16[33,8,512]{2,1,0:T(8,128)(2,1)S(1)}, u32[]{:S(2)}, u32[]{:S(2)}) %collective-permute-start.2) | collective-permute-done | bytes 270368 | tf_op jit(solution)/shard_map/ppermute | solution.py:389
  21.5 0.0 collective-permute-done.3.refs_7_
  21.5 0.0 collective-permute-done.refs_4_
  21.5 0.0 collective-permute-done.1.refs_5_
  21.5 10.1 %step.3 = (bf16[32,256,512]{2,1,0:T(8,128)(2,1)S(1)}, bf16[33,32,512]{2,1,0:T(8,128)(2,1)S(1)}, bf16[33,32,512]{2,1,0:T(8,128)(2,1)S(1)}, bf16[33,8,512]{2,1,0:T...) custom-call(s32[2]{0:T(128)S(1)} %pad_add_fusion.refs_0_.parity, ...), custom_call_target="tpu_custom_call" | custom-call | tf_op jit(solution)/shard_map/step/pallas_call | solution.py:32
  31.6 0.7 collective-permute-start.4
  32.3 3.5 %collective-permute-start.5 = (bf16[33,32,512]{2,1,0:T(8,128)(2,1)S(1)}, bf16[33,32,512]{2,1,0:T(8,128)(2,1)S(1)}, u32[]{:S(2)}, u32[]{:S(2)}) collective-permute-start(bf16[33,32,512]{2,1,0:T(8,128)(2,1)S(1)} %get-tuple-element.62), channel_id=1, source_target_pairs={{0,4},{4,0},{8,12},{12,8},{16,20},{20,16},{24,28},{28,24},{1,5},{5... | collective-permute-start | bytes 3244040 | tf_op jit(solution)/shard_map/ppermute | solution.py:388
  35.8 6.8 %collective-permute-start.6 = (bf16[33,8,512]{2,1,0:T(8,128)(2,1)S(1)}, bf16[33,8,512]{2,1,0:T(8,128)(2,1)S(1)}, u32[]{:S(2)}, u32[]{:S(2)}) collective-permute-start(bf16[33,8,512]{2,1,0:T(8,128)(2,1)S(1)} %get-tuple-element.63), channel_id=1, source_target_pairs={{0,1},{1,0},{2,3},{3,2},{4,5},{5,4},{6,7},{7,6},{8,9},{9,8},{10,11... | collective-permute-start | bytes 811016 | tf_op jit(solution)/shard_map/ppermute | solution.py:389
  42.5 0.7 collective-permute-start.7
  43.2 13.2 %all_to_all.33 = f32[32,1,128]{2,1,0:T(1,128)S(1)} all-to-all(f32[32,1,128]{2,1,0:T(1,128)S(1)} %bitcast.25), channel_id=1, replica_groups=mesh['gy'=8,'gx'=4] {'gy','gx'}, dimensions={0} | all-to-all | bytes 32768 | tf_op jit(solution)/shard_map/all_to_all | solution.py:467
  56.4 0.0 collective-permute-done.6.refs_9_
  56.4 0.0 collective-permute-done.7.refs_10_
  56.4 0.0 collective-permute-done.4.refs_7_
  56.4 0.0 collective-permute-done.5.refs_8_
  56.4 10.2 %step.4 = (bf16[32,256,512]{2,1,0:T(8,128)(2,1)S(1)}, bf16[33,32,512]{2,1,0:T(8,128)(2,1)S(1)}, bf16[33,32,512]{2,1,0:T(8,128)(2,1)S(1)}, bf16[33,8,512]{2,1,0:T...) custom-call(s32[2]{0:T(128)S(1)} %pad_add_fusion.refs_0_.parity, ...), custom_call_target="tpu_custom_call" | custom-call | tf_op jit(solution)/shard_map/step/pallas_call | solution.py:32
  66.6 0.7 collective-permute-start.8
  67.3 1.9 %collective-permute-start.9 = (bf16[33,32,512]{2,1,0:T(8,128)(2,1)S(1)}, bf16[33,32,512]{2,1,0:T(8,128)(2,1)S(1)}, u32[]{:S(2)}, u32[]{:S(2)}) collective-permute-start(bf16[33,32,512]{2,1,0:T(8,128)(2,1)S(1)} %get-tuple-element.71), channel_id=1, source_target_pairs={{0,4},{4,0},{8,12},{12,8},{16,20},{20,16},{24,28},{28,24},{1,5},{5... | collective-permute-start | bytes 3244040 | tf_op jit(solution)/shard_map/ppermute | solution.py:388
  69.3 0.6 collective-permute-start.10
  69.9 0.7 collective-permute-start.11
  70.6 14.4 %all_to_all.34 = f32[32,1,128]{2,1,0:T(1,128)S(1)} all-to-all(f32[32,1,128]{2,1,0:T(1,128)S(1)} %bitcast.24), channel_id=1, replica_groups=mesh['gy'=8,'gx'=4] {'gy','gx'}, dimensions={0} | all-to-all | bytes 32768 | tf_op jit(solution)/shard_map/all_to_all | solution.py:467
  84.9 0.0 collective-permute-done.10.refs_9_
  84.9 0.0 collective-permute-done.11.refs_10_
  85.0 0.0 collective-permute-done.8.refs_7_
  85.0 0.0 collective-permute-done.9.refs_8_
  85.0 9.8 %step.5 = (f32[256,128]{1,0:T(8,128)S(1)}, f32[256,128]{1,0:T(8,128)S(1)}, f32[256,128]{1,0:T(8,128)S(1)}, f32[32,128]{1,0:T(8,128)}) custom-call(s32[2]{0:T(128)S(1)} %pad_add_fusion.refs_0_.parity, f32[32]{0:T(128)S(1)} %copy-done.7, f32[32,128]{1,0:T(8,128)S(1)} %bitcast.21, f32[256,128]{1,0:T(8,128)S(1)} %get-tuple-element.66.refs_3_, ...), custom_call_target="tpu_custom_call" | custom-call | tf_op jit(solution)/shard_map/step/pallas_call | solution.py:32
  94.7 2.9 %all-to-all-start.2 = ((f32[32,1,128]{2,1,0:T(1,128)}), f32[32,1,128]{2,1,0:T(1,128)S(1)}, u32[]{:S(2)}, u32[]{:S(2)}) async-start(f32[32,1,128]{2,1,0:T(1,128)} %bitcast.12), calls=%async_computation.2 | async-start | bytes 32768 | tf_op jit(solution)/shard_map/all_to_all | solution.py:467
  97.6 1.1 %layout.1 = (f32[32,8,32]{2,1,0:T(8,128)S(1)}, f32[32,8,32]{2,1,0:T(8,128)S(1)}, f32[32,8,32]{2,1,0:T(8,128)}) custom-call(f32[256,128]{1,0:T(8,128)S(1)} %get-tuple-element.75.mean, f32[256,128]{1,0:T(8,128)S(1)} %get-tuple-element.76.res, f32[256,128]{1,0:T(8,128)S(1)} %get-tuple-element.77.log_pred), custom_call_target="tpu_custom_call" | custom-call | tf_op jit(solution)/shard_map/layout/pallas_call | solution.py:32
  98.8 6.0 %all-to-all-done.2 = f32[32,1,128]{2,1,0:T(1,128)S(1)} async-done(((f32[32,1,128]{2,1,0:T(1,128)}), f32[32,1,128]{2,1,0:T(1,128)S(1)}, u32[]{:S(2)}, u32[]{:S(2)}) %all-to-all-start.2) | async-done | bytes 16416 | tf_op jit(solution)/shard_map/all_to_all | solution.py:467
  104.7 0.8 final.1
  (9 shorter events, 0.0 us)
Async XLA Ops:
  0.7 0.9 copy-start.1
  1.6 7.6 %copy-start = (bf16[32,8,32,512]{3,2,1,0:T(8,128)(2,1)S(1)}, bf16[32,8,32,512]{3,2,1,0:T(8,128)(2,1)}, u32[]{:S(2)}) copy-start(bf16[32,8,32,512]{3,2,1,0:T(8,128)(2,1)} %prior.1) | copy-start | bytes 25165828
  4.0 17.5 %collective-permute-start = (bf16[33,32,512]{2,1,0:T(8,128)(2,1)S(1)}, bf16[33,32,512]{2,1,0:T(8,128)(2,1)S(1)}, u32[]{:S(2)}, u32[]{:S(2)}) collective-permute-start(bf16[33,32,512]{2,1,0:T(8,128)(2,1)S(1)} %get-tuple-element.44), channel_id=1, source_target_pairs={{4,8},{8,4},{12,16},{16,12},{20,24},{24,20},{5,9},{9,5},{13,17},{1... | collective-permute-start | bytes 3244040 | tf_op jit(solution)/shard_map/ppermute | solution.py:387
  4.9 16.6 %collective-permute-start.1 = (bf16[33,32,512]{2,1,0:T(8,128)(2,1)S(1)}, bf16[33,32,512]{2,1,0:T(8,128)(2,1)S(1)}, u32[]{:S(2)}, u32[]{:S(2)}) collective-permute-start(bf16[33,32,512]{2,1,0:T(8,128)(2,1)S(1)} %get-tuple-element.45), channel_id=1, source_target_pairs={{0,4},{4,0},{8,12},{12,8},{16,20},{20,16},{24,28},{28,24},{1,5},{5... | collective-permute-start | bytes 3244040 | tf_op jit(solution)/shard_map/ppermute | solution.py:388
  9.3 5.0 %copy-start.2 = (f32[32,8,32]{2,1,0:T(8,128)S(1)}, f32[32,8,32]{2,1,0:T(8,128)}, u32[]{:S(2)}) copy-start(f32[32,8,32]{2,1,0:T(8,128)} %mean.3) | copy-start | bytes 98308
  9.3 5.0 %copy-start.3 = (f32[4,32,8,32]{3,2,1,0:T(8,128)S(1)}, f32[4,32,8,32]{3,2,1,0:T(8,128)}, u32[]{:S(2)}) copy-start(f32[4,32,8,32]{3,2,1,0:T(8,128)} %refs_6_.1) | copy-start | bytes 393220
  9.3 5.0 %copy-start.4 = (f32[32,8,32]{2,1,0:T(8,128)S(1)}, f32[32,8,32]{2,1,0:T(8,128)}, u32[]{:S(2)}) copy-start(f32[32,8,32]{2,1,0:T(8,128)} %refs_5_.1) | copy-start | bytes 98308
  9.3 5.1 %copy-start.5 = (s32[4,8,32]{2,1,0:T(8,128)S(1)}, s32[4,8,32]{2,1,0:T(8,128)}, u32[]{:S(2)}) copy-start(s32[4,8,32]{2,1,0:T(8,128)} %refs_8_.1) | copy-start | bytes 12292
  9.3 5.1 %copy-start.6 = (f32[4,512]{1,0:T(4,128)S(1)}, f32[4,512]{1,0:T(4,128)}, u32[]{:S(2)}) copy-start(f32[4,512]{1,0:T(4,128)} %refs_7_.1) | copy-start | bytes 24580
  9.3 5.0 %copy-start.7 = (f32[32]{0:T(128)S(1)}, f32[32]{0:T(128)}, u32[]{:S(2)}) copy-start(f32[32]{0:T(128)} %refs_1_.7) | copy-start | bytes 388
  9.3 5.0 %copy-start.8 = (f32[4]{0:T(128)S(1)}, f32[4]{0:T(128)}, u32[]{:S(2)}) copy-start(f32[4]{0:T(128)} %refs_1_.4) | copy-start | bytes 52
  9.3 5.0 %copy-start.9 = (f32[32]{0:T(128)S(1)}, f32[32]{0:T(128)}, u32[]{:S(2)}) copy-start(f32[32]{0:T(128)} %param.16) | copy-start | bytes 388
  12.1 9.4 %collective-permute-start.2 = (bf16[33,8,512]{2,1,0:T(8,128)(2,1)S(1)}, bf16[33,8,512]{2,1,0:T(8,128)(2,1)S(1)}, u32[]{:S(2)}, u32[]{:S(2)}) collective-permute-start(bf16[33,8,512]{2,1,0:T(8,128)(2,1)S(1)} %get-tuple-element.46), channel_id=1, source_target_pairs={{0,1},{1,0},{2,3},{3,2},{4,5},{5,4},{6,7},{7,6},{8,9},{9,8},{10,11... | collective-permute-start | bytes 811016 | tf_op jit(solution)/shard_map/ppermute | solution.py:389
  13.6 7.9 %collective-permute-start.3 = (bf16[33,8,512]{2,1,0:T(8,128)(2,1)S(1)}, bf16[33,8,512]{2,1,0:T(8,128)(2,1)S(1)}, u32[]{:S(2)}, u32[]{:S(2)}) collective-permute-start(bf16[33,8,512]{2,1,0:T(8,128)(2,1)S(1)} %get-tuple-element.47), channel_id=1, source_target_pairs={{1,2},{2,1},{5,6},{6,5},{9,10},{10,9},{13,14},{14,13},{17,18},{18,... | collective-permute-start | bytes 811016 | tf_op jit(solution)/shard_map/ppermute | solution.py:390
  31.6 24.8 %collective-permute-start.4 = (bf16[33,32,512]{2,1,0:T(8,128)(2,1)S(1)}, bf16[33,32,512]{2,1,0:T(8,128)(2,1)S(1)}, u32[]{:S(2)}, u32[]{:S(2)}) collective-permute-start(bf16[33,32,512]{2,1,0:T(8,128)(2,1)S(1)} %get-tuple-element.61), channel_id=1, source_target_pairs={{4,8},{8,4},{12,16},{16,12},{20,24},{24,20},{5,9},{9,5},{13,17},{1... | collective-permute-start | bytes 3244040 | tf_op jit(solution)/shard_map/ppermute | solution.py:387
  32.3 24.1 %collective-permute-start.5 = (bf16[33,32,512]{2,1,0:T(8,128)(2,1)S(1)}, bf16[33,32,512]{2,1,0:T(8,128)(2,1)S(1)}, u32[]{:S(2)}, u32[]{:S(2)}) collective-permute-start(bf16[33,32,512]{2,1,0:T(8,128)(2,1)S(1)} %get-tuple-element.62), channel_id=1, source_target_pairs={{0,4},{4,0},{8,12},{12,8},{16,20},{20,16},{24,28},{28,24},{1,5},{5... | collective-permute-start | bytes 3244040 | tf_op jit(solution)/shard_map/ppermute | solution.py:388
  35.8 20.6 %collective-permute-start.6 = (bf16[33,8,512]{2,1,0:T(8,128)(2,1)S(1)}, bf16[33,8,512]{2,1,0:T(8,128)(2,1)S(1)}, u32[]{:S(2)}, u32[]{:S(2)}) collective-permute-start(bf16[33,8,512]{2,1,0:T(8,128)(2,1)S(1)} %get-tuple-element.63), channel_id=1, source_target_pairs={{0,1},{1,0},{2,3},{3,2},{4,5},{5,4},{6,7},{7,6},{8,9},{9,8},{10,11... | collective-permute-start | bytes 811016 | tf_op jit(solution)/shard_map/ppermute | solution.py:389
  42.5 13.8 %collective-permute-start.7 = (bf16[33,8,512]{2,1,0:T(8,128)(2,1)S(1)}, bf16[33,8,512]{2,1,0:T(8,128)(2,1)S(1)}, u32[]{:S(2)}, u32[]{:S(2)}) collective-permute-start(bf16[33,8,512]{2,1,0:T(8,128)(2,1)S(1)} %get-tuple-element.64), channel_id=1, source_target_pairs={{1,2},{2,1},{5,6},{6,5},{9,10},{10,9},{13,14},{14,13},{17,18},{18,... | collective-permute-start | bytes 811016 | tf_op jit(solution)/shard_map/ppermute | solution.py:390
  66.6 18.4 %collective-permute-start.8 = (bf16[33,32,512]{2,1,0:T(8,128)(2,1)S(1)}, bf16[33,32,512]{2,1,0:T(8,128)(2,1)S(1)}, u32[]{:S(2)}, u32[]{:S(2)}) collective-permute-start(bf16[33,32,512]{2,1,0:T(8,128)(2,1)S(1)} %get-tuple-element.70), channel_id=1, source_target_pairs={{4,8},{8,4},{12,16},{16,12},{20,24},{24,20},{5,9},{9,5},{13,17},{1... | collective-permute-start | bytes 3244040 | tf_op jit(solution)/shard_map/ppermute | solution.py:387
  67.3 17.6 %collective-permute-start.9 = (bf16[33,32,512]{2,1,0:T(8,128)(2,1)S(1)}, bf16[33,32,512]{2,1,0:T(8,128)(2,1)S(1)}, u32[]{:S(2)}, u32[]{:S(2)}) collective-permute-start(bf16[33,32,512]{2,1,0:T(8,128)(2,1)S(1)} %get-tuple-element.71), channel_id=1, source_target_pairs={{0,4},{4,0},{8,12},{12,8},{16,20},{20,16},{24,28},{28,24},{1,5},{5... | collective-permute-start | bytes 3244040 | tf_op jit(solution)/shard_map/ppermute | solution.py:388
  69.3 15.7 %collective-permute-start.10 = (bf16[33,8,512]{2,1,0:T(8,128)(2,1)S(1)}, bf16[33,8,512]{2,1,0:T(8,128)(2,1)S(1)}, u32[]{:S(2)}, u32[]{:S(2)}) collective-permute-start(bf16[33,8,512]{2,1,0:T(8,128)(2,1)S(1)} %get-tuple-element.72), channel_id=1, source_target_pairs={{0,1},{1,0},{2,3},{3,2},{4,5},{5,4},{6,7},{7,6},{8,9},{9,8},{10,11... | collective-permute-start | bytes 811016 | tf_op jit(solution)/shard_map/ppermute | solution.py:389
  69.9 15.1 %collective-permute-start.11 = (bf16[33,8,512]{2,1,0:T(8,128)(2,1)S(1)}, bf16[33,8,512]{2,1,0:T(8,128)(2,1)S(1)}, u32[]{:S(2)}, u32[]{:S(2)}) collective-permute-start(bf16[33,8,512]{2,1,0:T(8,128)(2,1)S(1)} %get-tuple-element.73), channel_id=1, source_target_pairs={{1,2},{2,1},{5,6},{6,5},{9,10},{10,9},{13,14},{14,13},{17,18},{18,... | collective-permute-start | bytes 811016 | tf_op jit(solution)/shard_map/ppermute | solution.py:390
  94.7 10.0 %all-to-all-start.2 = ((f32[32,1,128]{2,1,0:T(1,128)}), f32[32,1,128]{2,1,0:T(1,128)S(1)}, u32[]{:S(2)}, u32[]{:S(2)}) async-start(f32[32,1,128]{2,1,0:T(1,128)} %bitcast.12), calls=%async_computation.2 | async-start | bytes 32768 | tf_op jit(solution)/shard_map/all_to_all | solution.py:467

commit v2 on v1

--- a/solution.py
+++ b/solution.py
@@ -12,10 +12,11 @@
 step_level = 0.2
 gap_eps = 1e-06
 LANES = 128
-GROUP = 4
-PARTS = 3
-LEFT = (0, 0, 1, 0, 1, 2)
-RIGHT = (0, 1, 0, 2, 1, 0)
+GROUP = 2
+UNROLL = 4
+PARTS = 2
+LEFT = (0, 0, 1)
+RIGHT = (0, 1, 0)
 F32 = jnp.float32
 BF16 = jnp.bfloat16
 LOG2E = 1.0 / math.log(2.0)
@@ -28,13 +29,14 @@
     return jax.ShapeDtypeStruct(dims, dtype)
 
 
-def call(body, name, args, in_specs, out_shape, scratch=(), mib=8, out_specs=None):
+def call(body, name, args, in_specs, out_shape, scratch=(), mib=8, out_specs=None, alias=None):
     return pl.pallas_call(
         body,
         out_shape=out_shape,
         in_specs=in_specs,
         out_specs=out_specs or tuple(VMEM for _ in out_shape),
         scratch_shapes=list(scratch),
+        input_output_aliases=alias or {},
         compiler_params=pltpu.CompilerParams(vmem_limit_bytes=mib * 1024 * 1024),
         name=name,
     )(*args)
@@ -55,6 +57,16 @@
 
 def iota(dims, axis):
     return lax.broadcasted_iota(jnp.int32, dims, axis)
+
+
+def plan(dims, K):
+    J, TR, TC, R, ND = dims
+    rim = TC
+    cols = rim + TC
+    taste = cols + 2 * TR
+    base = taste + len(LEFT) * GROUP * K
+    assert TR * TC == 2 * LANES and base + 2 * GROUP <= LANES
+    return rim, cols, taste, base
 
 
 def side_columns(x, lo):
@@ -92,8 +104,9 @@
     M = TR * TC
     lo = LANES - J
     (parity, scale_s, spill, rates, mean, shares, chars, draws, links) = refs[:9]
-    (Wl, Wc, T4, dsel, cnt, rate, ispill, table, logobs) = refs[9:18]
-    taste, a_s = refs[18:]
+    (Wl, Wc, Lf, F, dsel, cnt, rate, ispill, table, logobs) = refs[9:19]
+    taste, a_s = refs[19:]
+    rim_at, cols_at, taste_at, base_at = plan(dims, K)
     py, px = parity[0], parity[1]
 
     columns = links[...].astype(F32).reshape(4 * TR, TC)
@@ -108,13 +121,18 @@
     me = iota((M, LANES), 0)
     lane = iota((M, LANES), 1)
     r, c = me // TC, me % TC
-    for b in range(M // LANES):
-        other = lane + b * LANES
+
+    def inside(other):
         w = jnp.where(other == me - TC, a_s[0], 0.0)
         w = w + jnp.where(other == me + TC, a_s[1], 0.0)
         w = w + jnp.where((other == me - 1) & (c > 0), a_s[2], 0.0)
-        w = w + jnp.where((other == me + 1) & (c < TC - 1), a_s[3], 0.0)
-        Wl[:, b * LANES : (b + 1) * LANES] = w.astype(BF16)
+        return w + jnp.where((other == me + 1) & (c < TC - 1), a_s[3], 0.0)
+
+    for b in range(M // LANES):
+        Wl[:, b * LANES : (b + 1) * LANES] = inside(lane + b * LANES).astype(BF16)
+    start = jnp.where(me < LANES, 0, LANES - TC)
+    Lf[...] = inside(lane + start).astype(BF16)
+    fixed = jnp.where(lane < TC, inside(lane + LANES + start), 0.0)
     north = jnp.where(r == 0, a_s[0], 0.0)
     south = jnp.where(r == TR - 1, a_s[1], 0.0)
     west = jnp.where(c == 0, a_s[2], 0.0)
@@ -123,6 +141,12 @@
     near_row = jnp.where(py == 1, north, south)
     near_col = jnp.where(px == 1, west, east)
     far_col = jnp.where(px == 1, east, west)
+    fixed = (
+        fixed
+        + jnp.where(lane == rim_at + c, north + south, 0.0)
+        + jnp.where(lane == cols_at + r, near_col, 0.0)
+        + jnp.where(lane == cols_at + TR + r, far_col, 0.0)
+    )
     Wc[...] = (
         jnp.where(lane == c, far_row, 0.0)
         + jnp.where(lane == TC + c, near_row, 0.0)
@@ -143,29 +167,32 @@
     parts = kernel_parts(taste[...] * count, PARTS)
     width = GROUP * K
     src = iota((LANES, LANES), 0)
-    dst = iota((LANES, LANES), 1)
+    dst = iota((LANES, LANES), 1) - taste_at
     term, inner = dst // width, dst % width
     for g in range(J // GROUP):
         wanted = (inner // GROUP) * J + g * GROUP + inner % GROUP
-        hit = (src == wanted) & (term < len(LEFT))
-        total = jnp.zeros((M, LANES), F32)
+        hit = (src == wanted) & (dst >= 0) & (dst < base_at - taste_at)
+        total = fixed
         for p in range(PARTS):
             which = functools.reduce(jnp.logical_or, [term == t for t, l in enumerate(LEFT) if l == p])
             total = total + dot(parts[p], jnp.where(hit & which, 1.0, 0.0).astype(BF16))
-        T4[g] = total.astype(BF16)
+        F[g] = total.astype(BF16)
 
     d_parts = kernel_parts(draws[...], PARTS)
     held = jnp.concatenate([p.astype(F32) for p in d_parts], axis=0)
     held = jnp.concatenate([held, jnp.zeros((LANES - PARTS * K, R), F32)], axis=0).astype(BF16)
-    src = iota((LANES, LANES), 1)
-    dst = iota((LANES, LANES), 0)
+    deep = LANES - taste_at
+    src = iota((deep, LANES), 1)
+    dst = iota((deep, LANES), 0)
     term, inner = dst // width, dst % width
+    line = iota((deep, R), 0) - (base_at - taste_at)
     for q in range(GROUP):
-        hit = jnp.zeros((LANES, LANES), jnp.bool_)
+        hit = jnp.zeros((deep, LANES), jnp.bool_)
         for t, p in enumerate(RIGHT):
             hit = hit | ((term == t) & (src == p * K + inner // GROUP))
         hit = hit & (inner % GROUP == q)
-        dsel[q] = dot(jnp.where(hit, 1.0, 0.0).astype(BF16), held).astype(BF16)
+        ones = jnp.where((line == q) | (line == GROUP + q), 1.0, 0.0)
+        dsel[q] = (dot(jnp.where(hit, 1.0, 0.0).astype(BF16), held) + ones).astype(BF16)
 
 
 def columns_kernel(dims, parity, mean, state, pC, pD):
@@ -177,15 +204,10 @@
     col = jnp.where(line < TR, (1 - px) * (TC - 1), px * (TC - 1))
     pick = jnp.where(iota((2 * TR, M), 1) == (line % TR) * TC + col, 1.0, 0.0).astype(BF16)
 
-    def body(g, carry):
-        for q in range(GROUP):
-            j = g * GROUP + q
-            found = dot(pick, state[j]).astype(BF16)
-            pC[j] = found[:TR]
-            pD[j] = found[TR:]
-        return carry
-
-    lax.fori_loop(0, J // GROUP, body, 0)
+    for j in range(J):
+        found = dot(pick, state[j]).astype(BF16)
+        pC[j] = found[:TR]
+        pD[j] = found[TR:]
     west, east = [], []
     for i in range(TR):
         block = side_columns(mean[:, i, :], lo)
@@ -197,7 +219,7 @@
     plane(pD, J, jnp.where(px == 0, west, east))
 
 
-def step_kernel(dims, first, last, *refs):
+def step_kernel(dims, K, first, last, *refs):
     J, TR, TC, R, ND = dims
     M = TR * TC
     lo = LANES - J
@@ -207,17 +229,17 @@
     if not first:
         mall, res_in, mh_in = refs[:3]
         refs = refs[3:]
-    mean_in, state, hB, hA, hC, hD, Wl, Wc, T4, dsel, cnt, rate, ispill, logobs = refs[:14]
-    refs = refs[14:]
+    mean_in, state, hB, hA, hC, hD, Wl, Wc, Lf, F, dsel, cnt, rate, ispill, logobs = refs[:15]
+    refs = refs[15:]
     if last:
         mean_out, res_out, log_out, mloc = refs[:4]
         refs = refs[4:]
     else:
         state_out, pB, pA, pC, pD, mean_out, res_out, mh_out, mloc = refs[:9]
         refs = refs[9:]
-    E, den, Wcb, W4b, S_ref, sc_ref = refs[:6]
+    E, den, W, S_ref, sc_ref = refs[:5]
     if not last:
-        colf = refs[6]
+        colf = refs[5]
 
     rim = []
     for h in (hB, hA, hC, hD):
@@ -241,31 +263,45 @@
         acc = acc + dot(Wc[...], part)
     scaled = (mean * cnt[...] + rate[...] * acc) * ispill[...]
     b_hi, b_mid = kernel_parts(scaled, 2)
-    Wcb[...] = Wc[...] + b_hi
+    src = iota((LANES, LANES), 0) - lo
+    dst = iota((LANES, LANES), 1)
+    spot = 2 * GROUP * (src // GROUP) + src % GROUP
+    hi_to = jnp.where((src >= 0) & (dst == spot), 1.0, 0.0).astype(BF16)
+    mid_to = jnp.where((src >= 0) & (dst == spot + GROUP), 1.0, 0.0).astype(BF16)
+    mixed = dot(b_hi, hi_to) + dot(b_mid, mid_to)
+    base_at = plan(dims, K)[3]
+    full_lane = iota((M, LANES), 1)
+    in_base = (full_lane >= base_at) & (full_lane < base_at + 2 * GROUP)
     for g in range(J // GROUP):
-        W4b[g] = T4[g] + b_mid
+        moved = pltpu.roll(mixed, (base_at - 2 * GROUP * g) % LANES, axis=1)
+        W[g] = F[g] + jnp.where(in_base, moved, 0.0).astype(BF16)
     sc_ref[...] = LOG2E / cnt[...]
     den[...] = jnp.ones_like(den)
 
-    row_id = iota((J, R), 0)
-    zeros_mid = jnp.zeros((lo - 2 * (TR + TC), R), BF16)
-
-    def pass_one(g, carry):
-        for q in range(GROUP):
-            j = g * GROUP + q
-            onehot = jnp.where(row_id == j, 1.0, 0.0).astype(BF16)
-            cd = jnp.concatenate([hC[j].astype(F32), hD[j].astype(F32)], axis=0).astype(BF16)
-            rhs = jnp.concatenate([hB[j], hA[j], cd, zeros_mid, onehot, dsel[q, :lo, :], onehot], axis=0)
-            lhs = jnp.concatenate([Wcb[...], W4b[g]], axis=1)
-            total = dot(Wl[...], state[j]) + dot(lhs, rhs)
-            factor = sc_ref[...] * spill[j]
-            factor = jnp.concatenate([factor] * (R // LANES), axis=1)
-            e = jnp.exp2(total * factor)
-            E[j] = e
-            den[...] += e
+    odd = parity[0] == 1
+    span = LANES + TC
+
+    def pass_one(trip, carry):
+        for n in range(UNROLL):
+            g = trip * UNROLL + n
+            for q in range(GROUP):
+                j = g * GROUP + q
+                cd = jnp.concatenate([hC[j].astype(F32), hD[j].astype(F32)], axis=0).astype(BF16)
+                far, close = hB[j], hA[j]
+                rims = (jnp.where(odd, close, far), jnp.where(odd, far, close))
+                for b in range(2):
+                    rows = slice(b * LANES, (b + 1) * LANES)
+                    local_rows = state[j, b * (M - span) : b * (M - span) + span, :]
+                    rhs = jnp.concatenate([local_rows, rims[b], cd, dsel[q]], axis=0)
+                    lhs = jnp.concatenate([Lf[rows, :], W[g, rows, :]], axis=1)
+                    factor = sc_ref[rows, :] * spill[j]
+                    factor = jnp.concatenate([factor] * (R // LANES), axis=1)
+                    e = jnp.exp2(dot(lhs, rhs) * factor)
+                    E[j, rows, :] = e
+                    den[rows, :] += e
         return carry
 
-    lax.fori_loop(0, J // GROUP, pass_one, 0)
+    lax.fori_loop(0, J // (GROUP * UNROLL), pass_one, 0)
 
     lane = iota((TC, LANES), 1)
 
@@ -399,7 +435,7 @@
     )
     halos = exchange(pB, pA, pC, pD)
 
-    Wl, Wc, T4, dsel, cnt, rate, ispill, mean, logobs = call(
+    Wl, Wc, Lf, F, dsel, cnt, rate, ispill, mean, logobs = call(
         functools.partial(prep_kernel, dims, K),
         "prep",
         (
@@ -417,8 +453,9 @@
         (
             shape((M, M), BF16),
             shape((M, LANES), BF16),
+            shape((M, LANES), BF16),
             shape((J // GROUP, M, LANES), BF16),
-            shape((GROUP, LANES, R), BF16),
+            shape((GROUP, LANES - plan(dims, K)[2], R), BF16),
             table,
             shape((1, LANES)),
             shape((1, LANES)),
@@ -435,7 +472,7 @@
         first, last = iteration == 0, iteration + 1 == ITERS
         moving = () if first else (peaks[-1], res, rim)
         args = (parity, spill_rate) + moving + (mean, state) + halos
-        args = args + (Wl, Wc, T4, dsel, cnt, rate, ispill, logobs)
+        args = args + (Wl, Wc, Lf, F, dsel, cnt, rate, ispill, logobs)
         if last:
             outs = (table, table, table, peak_shape)
         else:
@@ -443,7 +480,6 @@
         scratch = [
             pltpu.VMEM((J, M, R), F32),
             pltpu.VMEM((M, R), F32),
-            pltpu.VMEM((M, LANES), BF16),
             pltpu.VMEM((J // GROUP, M, LANES), BF16),
             pltpu.VMEM((M, LANES), F32),
             pltpu.VMEM((M, LANES), F32),
@@ -451,13 +487,14 @@
         if not last:
             scratch.append(pltpu.VMEM((2, J, TR, R), F32))
         out = call(
-            functools.partial(step_kernel, dims, first, last),
+            functools.partial(step_kernel, dims, K, first, last),
             "step",
             args,
             [SMEM, SMEM] + [VMEM] * (len(args) - 2),
             outs,
             scratch,
-            mib=23,
+            mib=22,
+            alias={} if first or last else {6: 0},
         )
         if last:
             mean, res, log_pred, peak = out

time: 106 us -> 97.7 us (0.922)
  Pallas kernels: 39 us -> 31.1 us
    pallas_call x8, Pallas kernels: 39 us -> 31.1 us  [call(): pl.pallas_call(body, out_shape=out_shape, in_specs=in_specs, out_specs=ou...]
    ppermute x3, starting transfers between devices: 8.92 us -> 7.84 us  [exchange(): lax.ppermute(pC, 'gx', near_x)]
  transfers between devices with their start and end apart: 13 -> 13, of which waited for: 2 -> 2; matrix products, arithmetic and copies ran while one was open for 0% -> 0% of each run, Pallas kernels for 6% -> 5%
where the time goes in v2:
time: 97.7 us; the launch traced here: 97.4 us
  Pallas kernels  31.1 us (32%)
  blocking collectives  27.6 us (28%)
  starting transfers between devices  25.9 us (27%)
  waiting for transfers between devices  11 us (11%)
    pallas_call x8, Pallas kernels, call(): pl.pallas_call(body, out_shape=out_shape, in_specs=in_specs, out_specs=ou...  31.1 us
    all_to_all x2, blocking collectives, local(): peaks.append(lax.all_to_all(peak, ('gy', 'gx'), 0, 0, tiled=True))  27.6 us
    ppermute x3, starting transfers between devices, exchange(): lax.ppermute(pA, 'gy', near_y)  10.8 us
    ppermute x3, starting transfers between devices, exchange(): lax.ppermute(pC, 'gx', near_x)  7.84 us
    all_to_all x1, waiting for transfers between devices, local(): peaks.append(lax.all_to_all(peak, ('gy', 'gx'), 0, 0, tiled=True))  5.98 us
    ppermute x3, waiting for transfers between devices, exchange(): lax.ppermute(pC, 'gx', near_x)  4.99 us
    all_to_all x1, starting transfers between devices, local(): peaks.append(lax.all_to_all(peak, ('gy', 'gx'), 0, 0, tiled=True))  2.89 us
    ppermute x3, starting transfers between devices, exchange(): lax.ppermute(pB, 'gy', far_y)  2.32 us
  transfers between devices with their start and end apart: 13, of which 2 were waited for; matrix products, arithmetic and copies ran while one was open for 0% of the time, Pallas kernels for 5%

profile of v2, /device:TPU:0, one launch (start us, length us, event | category | flops | bytes accessed | tf_op | source)
XLA Modules:
  0.0 97.4 jit_solution(4739789059245166895)
XLA Ops:
  0.6 0.1 pad_add_fusion.refs_0_.parity
  0.7 0.9 copy-done.1
  1.6 2.3 %rows.1 = (bf16[33,32,512]{2,1,0:T(8,128)(2,1)S(1)}, bf16[33,32,512]{2,1,0:T(8,128)(2,1)S(1)}) custom-call(s32[2]{0:T(128)S(1)} %pad_add_fusion.refs_0_.parity, f32[32,8,32]{2,1,0:T(8,128)S(1)} %copy-done.1, bf16[32,8,32,512]{3,2,1,0:T(8,128)(2,1)} %prior.1), custom_call_target="tpu_custom_call" | custom-call | tf_op jit(solution)/shard_map/rows/pallas_call | solution.py:33
  4.0 0.9 collective-permute-start
  4.9 4.4 %collective-permute-start.1 = (bf16[33,32,512]{2,1,0:T(8,128)(2,1)S(1)}, bf16[33,32,512]{2,1,0:T(8,128)(2,1)S(1)}, u32[]{:S(2)}, u32[]{:S(2)}) collective-permute-start(bf16[33,32,512]{2,1,0:T(8,128)(2,1)S(1)} %get-tuple-element.46), channel_id=1, source_target_pairs={{0,4},{4,0},{8,12},{12,8},{16,20},{20,16},{24,28},{28,24},{1,5},{5... | collective-permute-start | bytes 3244040 | tf_op jit(solution)/shard_map/ppermute | solution.py:424
  9.3 0.0 copy-start.5
  9.3 0.0 copy-start.6
  9.3 0.0 copy-start.7
  9.3 0.0 copy-start.8
  9.3 0.0 copy-start.9
  9.3 1.8 %columns.1 = (bf16[33,8,512]{2,1,0:T(8,128)(2,1)S(1)}, bf16[33,8,512]{2,1,0:T(8,128)(2,1)S(1)}) custom-call(s32[2]{0:T(128)S(1)} %pad_add_fusion.refs_0_.parity, f32[32,8,32]{2,1,0:T(8,128)S(1)} %copy-done.1, bf16[32,256,512]{2,1,0:T(8,128)(2,1)S(1)} %bitcast.17), custom_call_target="tpu_custom_call" | custom-call | tf_op jit(solution)/shard_map/columns/pallas_call | solution.py:33
  11.1 1.5 %collective-permute-start.2 = (bf16[33,8,512]{2,1,0:T(8,128)(2,1)S(1)}, bf16[33,8,512]{2,1,0:T(8,128)(2,1)S(1)}, u32[]{:S(2)}, u32[]{:S(2)}) collective-permute-start(bf16[33,8,512]{2,1,0:T(8,128)(2,1)S(1)} %get-tuple-element.47), channel_id=1, source_target_pairs={{0,1},{1,0},{2,3},{3,2},{4,5},{5,4},{6,7},{7,6},{8,9},{9,8},{10,11... | collective-permute-start | bytes 811016 | tf_op jit(solution)/shard_map/ppermute | solution.py:425
  12.6 0.7 collective-permute-start.3
  13.3 0.0 copy-done.2
  13.3 0.0 copy-done.3
  13.3 0.0 copy-done.4
  13.3 0.0 copy-done.5
  13.3 0.0 copy-done.6
  13.3 2.1 %prep.1 = (bf16[256,256]{1,0:T(8,128)(2,1)S(1)}, bf16[256,128]{1,0:T(8,128)(2,1)S(1)}, bf16[256,128]{1,0:T(8,128)(2,1)S(1)}, bf16[16,256,128]{2,1,0:T(8,128)(2,1...) custom-call(s32[2]{0:T(128)S(1)} %pad_add_fusion.refs_0_.parity, ...), custom_call_target="tpu_custom_call" | custom-call | tf_op jit(solution)/shard_map/prep/pallas_call | solution.py:33
  15.5 5.0 %collective-permute-done.2.refs_6_ = bf16[33,8,512]{2,1,0:T(8,128)(2,1)S(1)} collective-permute-done((bf16[33,8,512]{2,1,0:T(8,128)(2,1)S(1)}, bf16[33,8,512]{2,1,0:T(8,128)(2,1)S(1)}, u32[]{:S(2)}, u32[]{:S(2)}) %collective-permute-start.2) | collective-permute-done | bytes 270368 | tf_op jit(solution)/shard_map/ppermute | solution.py:425
  20.5 0.0 collective-permute-done.3.refs_7_
  20.5 0.0 collective-permute-done.refs_4_
  20.5 0.0 collective-permute-done.1.refs_5_
  20.5 7.7 %step.3 = (bf16[32,256,512]{2,1,0:T(8,128)(2,1)S(1)}, bf16[33,32,512]{2,1,0:T(8,128)(2,1)S(1)}, bf16[33,32,512]{2,1,0:T(8,128)(2,1)S(1)}, bf16[33,8,512]{2,1,0:T...) custom-call(s32[2]{0:T(128)S(1)} %pad_add_fusion.refs_0_.parity, ...), custom_call_target="tpu_custom_call" | custom-call | tf_op jit(solution)/shard_map/step/pallas_call | solution.py:33
  28.1 0.7 collective-permute-start.4
  28.9 4.5 %collective-permute-start.5 = (bf16[33,32,512]{2,1,0:T(8,128)(2,1)S(1)}, bf16[33,32,512]{2,1,0:T(8,128)(2,1)S(1)}, u32[]{:S(2)}, u32[]{:S(2)}) collective-permute-start(bf16[33,32,512]{2,1,0:T(8,128)(2,1)S(1)} %get-tuple-element.64), channel_id=1, source_target_pairs={{0,4},{4,0},{8,12},{12,8},{16,20},{20,16},{24,28},{28,24},{1,5},{5... | collective-permute-start | bytes 3244040 | tf_op jit(solution)/shard_map/ppermute | solution.py:424
  33.4 5.7 %collective-permute-start.6 = (bf16[33,8,512]{2,1,0:T(8,128)(2,1)S(1)}, bf16[33,8,512]{2,1,0:T(8,128)(2,1)S(1)}, u32[]{:S(2)}, u32[]{:S(2)}) collective-permute-start(bf16[33,8,512]{2,1,0:T(8,128)(2,1)S(1)} %get-tuple-element.65), channel_id=1, source_target_pairs={{0,1},{1,0},{2,3},{3,2},{4,5},{5,4},{6,7},{7,6},{8,9},{9,8},{10,11... | collective-permute-start | bytes 811016 | tf_op jit(solution)/shard_map/ppermute | solution.py:425
  39.1 0.7 collective-permute-start.7
  39.8 13.2 %all_to_all.33 = f32[32,1,128]{2,1,0:T(1,128)S(1)} all-to-all(f32[32,1,128]{2,1,0:T(1,128)S(1)} %bitcast.25), channel_id=1, replica_groups=mesh['gy'=8,'gx'=4] {'gy','gx'}, dimensions={0} | all-to-all | bytes 32768 | tf_op jit(solution)/shard_map/all_to_all | solution.py:504
  52.9 0.0 collective-permute-done.6.refs_9_
  52.9 0.0 collective-permute-done.7.refs_10_
  52.9 0.0 collective-permute-done.4.refs_7_
  53.0 0.0 collective-permute-done.5.refs_8_
  53.0 7.8 %step.4 = (bf16[32,256,512]{2,1,0:T(8,128)(2,1)S(1)}, bf16[33,32,512]{2,1,0:T(8,128)(2,1)S(1)}, bf16[33,32,512]{2,1,0:T(8,128)(2,1)S(1)}, bf16[33,8,512]{2,1,0:T...) custom-call(s32[2]{0:T(128)S(1)} %pad_add_fusion.refs_0_.parity, ...), custom_call_target="tpu_custom_call", output_to_operand_aliasing={{0}: (6, {})} | custom-call | tf_op jit(solution)/shard_map/step/pallas_call | solution.py:33
  60.8 0.7 collective-permute-start.8
  61.5 1.9 %collective-permute-start.9 = (bf16[33,32,512]{2,1,0:T(8,128)(2,1)S(1)}, bf16[33,32,512]{2,1,0:T(8,128)(2,1)S(1)}, u32[]{:S(2)}, u32[]{:S(2)}) collective-permute-start(bf16[33,32,512]{2,1,0:T(8,128)(2,1)S(1)} %get-tuple-element.73), channel_id=1, source_target_pairs={{0,4},{4,0},{8,12},{12,8},{16,20},{20,16},{24,28},{28,24},{1,5},{5... | collective-permute-start | bytes 3244040 | tf_op jit(solution)/shard_map/ppermute | solution.py:424
  63.5 0.6 collective-permute-start.10
  64.1 0.7 collective-permute-start.11
  64.8 14.4 %all_to_all.34 = f32[32,1,128]{2,1,0:T(1,128)S(1)} all-to-all(f32[32,1,128]{2,1,0:T(1,128)S(1)} %bitcast.24), channel_id=1, replica_groups=mesh['gy'=8,'gx'=4] {'gy','gx'}, dimensions={0} | all-to-all | bytes 32768 | tf_op jit(solution)/shard_map/all_to_all | solution.py:504
  79.1 0.0 collective-permute-done.10.refs_9_
  79.2 0.0 collective-permute-done.11.refs_10_
  79.2 0.0 collective-permute-done.8.refs_7_
  79.2 0.0 collective-permute-done.9.refs_8_
  79.2 7.4 %step.5 = (f32[256,128]{1,0:T(8,128)S(1)}, f32[256,128]{1,0:T(8,128)S(1)}, f32[256,128]{1,0:T(8,128)S(1)}, f32[32,128]{1,0:T(8,128)}) custom-call(s32[2]{0:T(128)S(1)} %pad_add_fusion.refs_0_.parity, f32[32]{0:T(128)S(1)} %copy-done.7, f32[32,128]{1,0:T(8,128)S(1)} %bitcast.21, f32[256,128]{1,0:T(8,128)S(1)} %get-tuple-element.68.refs_3_, ...), custom_call_target="tpu_custom_call" | custom-call | tf_op jit(solution)/shard_map/step/pallas_call | solution.py:33
  86.6 2.9 %all-to-all-start.2 = ((f32[32,1,128]{2,1,0:T(1,128)}), f32[32,1,128]{2,1,0:T(1,128)S(1)}, u32[]{:S(2)}, u32[]{:S(2)}) async-start(f32[32,1,128]{2,1,0:T(1,128)} %bitcast.12), calls=%async_computation.2 | async-start | bytes 32768 | tf_op jit(solution)/shard_map/all_to_all | solution.py:504
  89.5 1.1 %layout.1 = (f32[32,8,32]{2,1,0:T(8,128)S(1)}, f32[32,8,32]{2,1,0:T(8,128)S(1)}, f32[32,8,32]{2,1,0:T(8,128)}) custom-call(f32[256,128]{1,0:T(8,128)S(1)} %get-tuple-element.77.mean, f32[256,128]{1,0:T(8,128)S(1)} %get-tuple-element.78.res, f32[256,128]{1,0:T(8,128)S(1)} %get-tuple-element.79.log_pred), custom_call_target="tpu_custom_call" | custom-call | tf_op jit(solution)/shard_map/layout/pallas_call | solution.py:33
  90.6 6.0 %all-to-all-done.2 = f32[32,1,128]{2,1,0:T(1,128)S(1)} async-done(((f32[32,1,128]{2,1,0:T(1,128)}), f32[32,1,128]{2,1,0:T(1,128)S(1)}, u32[]{:S(2)}, u32[]{:S(2)}) %all-to-all-start.2) | async-done | bytes 16416 | tf_op jit(solution)/shard_map/all_to_all | solution.py:504
  96.6 0.8 final.1
  (9 shorter events, 0.0 us)
Async XLA Ops:
  0.7 0.9 copy-start.1
  1.6 7.6 %copy-start = (bf16[32,8,32,512]{3,2,1,0:T(8,128)(2,1)S(1)}, bf16[32,8,32,512]{3,2,1,0:T(8,128)(2,1)}, u32[]{:S(2)}) copy-start(bf16[32,8,32,512]{3,2,1,0:T(8,128)(2,1)} %prior.1) | copy-start | bytes 25165828
  4.0 16.5 %collective-permute-start = (bf16[33,32,512]{2,1,0:T(8,128)(2,1)S(1)}, bf16[33,32,512]{2,1,0:T(8,128)(2,1)S(1)}, u32[]{:S(2)}, u32[]{:S(2)}) collective-permute-start(bf16[33,32,512]{2,1,0:T(8,128)(2,1)S(1)} %get-tuple-element.45), channel_id=1, source_target_pairs={{4,8},{8,4},{12,16},{16,12},{20,24},{24,20},{5,9},{9,5},{13,17},{1... | collective-permute-start | bytes 3244040 | tf_op jit(solution)/shard_map/ppermute | solution.py:423
  4.9 15.6 %collective-permute-start.1 = (bf16[33,32,512]{2,1,0:T(8,128)(2,1)S(1)}, bf16[33,32,512]{2,1,0:T(8,128)(2,1)S(1)}, u32[]{:S(2)}, u32[]{:S(2)}) collective-permute-start(bf16[33,32,512]{2,1,0:T(8,128)(2,1)S(1)} %get-tuple-element.46), channel_id=1, source_target_pairs={{0,4},{4,0},{8,12},{12,8},{16,20},{20,16},{24,28},{28,24},{1,5},{5... | collective-permute-start | bytes 3244040 | tf_op jit(solution)/shard_map/ppermute | solution.py:424
  9.3 4.0 %copy-start.2 = (f32[32,8,32]{2,1,0:T(8,128)S(1)}, f32[32,8,32]{2,1,0:T(8,128)}, u32[]{:S(2)}) copy-start(f32[32,8,32]{2,1,0:T(8,128)} %mean.3) | copy-start | bytes 98308
  9.3 4.0 %copy-start.3 = (f32[4,32,8,32]{3,2,1,0:T(8,128)S(1)}, f32[4,32,8,32]{3,2,1,0:T(8,128)}, u32[]{:S(2)}) copy-start(f32[4,32,8,32]{3,2,1,0:T(8,128)} %refs_6_.1) | copy-start | bytes 393220
  9.3 4.0 %copy-start.4 = (f32[32,8,32]{2,1,0:T(8,128)S(1)}, f32[32,8,32]{2,1,0:T(8,128)}, u32[]{:S(2)}) copy-start(f32[32,8,32]{2,1,0:T(8,128)} %refs_5_.1) | copy-start | bytes 98308
  9.3 4.0 %copy-start.5 = (s32[4,8,32]{2,1,0:T(8,128)S(1)}, s32[4,8,32]{2,1,0:T(8,128)}, u32[]{:S(2)}) copy-start(s32[4,8,32]{2,1,0:T(8,128)} %refs_8_.1) | copy-start | bytes 12292
  9.3 4.0 %copy-start.6 = (f32[4,512]{1,0:T(4,128)S(1)}, f32[4,512]{1,0:T(4,128)}, u32[]{:S(2)}) copy-start(f32[4,512]{1,0:T(4,128)} %refs_7_.1) | copy-start | bytes 24580
  9.3 4.0 %copy-start.7 = (f32[32]{0:T(128)S(1)}, f32[32]{0:T(128)}, u32[]{:S(2)}) copy-start(f32[32]{0:T(128)} %refs_1_.7) | copy-start | bytes 388
  9.3 4.0 %copy-start.8 = (f32[4]{0:T(128)S(1)}, f32[4]{0:T(128)}, u32[]{:S(2)}) copy-start(f32[4]{0:T(128)} %refs_1_.4) | copy-start | bytes 52
  9.3 4.0 %copy-start.9 = (f32[32]{0:T(128)S(1)}, f32[32]{0:T(128)}, u32[]{:S(2)}) copy-start(f32[32]{0:T(128)} %param.16) | copy-start | bytes 388
  11.1 9.4 %collective-permute-start.2 = (bf16[33,8,512]{2,1,0:T(8,128)(2,1)S(1)}, bf16[33,8,512]{2,1,0:T(8,128)(2,1)S(1)}, u32[]{:S(2)}, u32[]{:S(2)}) collective-permute-start(bf16[33,8,512]{2,1,0:T(8,128)(2,1)S(1)} %get-tuple-element.47), channel_id=1, source_target_pairs={{0,1},{1,0},{2,3},{3,2},{4,5},{5,4},{6,7},{7,6},{8,9},{9,8},{10,11... | collective-permute-start | bytes 811016 | tf_op jit(solution)/shard_map/ppermute | solution.py:425
  12.6 7.9 %collective-permute-start.3 = (bf16[33,8,512]{2,1,0:T(8,128)(2,1)S(1)}, bf16[33,8,512]{2,1,0:T(8,128)(2,1)S(1)}, u32[]{:S(2)}, u32[]{:S(2)}) collective-permute-start(bf16[33,8,512]{2,1,0:T(8,128)(2,1)S(1)} %get-tuple-element.48), channel_id=1, source_target_pairs={{1,2},{2,1},{5,6},{6,5},{9,10},{10,9},{13,14},{14,13},{17,18},{18,... | collective-permute-start | bytes 811016 | tf_op jit(solution)/shard_map/ppermute | solution.py:426
  28.1 24.8 %collective-permute-start.4 = (bf16[33,32,512]{2,1,0:T(8,128)(2,1)S(1)}, bf16[33,32,512]{2,1,0:T(8,128)(2,1)S(1)}, u32[]{:S(2)}, u32[]{:S(2)}) collective-permute-start(bf16[33,32,512]{2,1,0:T(8,128)(2,1)S(1)} %get-tuple-element.63), channel_id=1, source_target_pairs={{4,8},{8,4},{12,16},{16,12},{20,24},{24,20},{5,9},{9,5},{13,17},{1... | collective-permute-start | bytes 3244040 | tf_op jit(solution)/shard_map/ppermute | solution.py:423
  28.9 24.1 %collective-permute-start.5 = (bf16[33,32,512]{2,1,0:T(8,128)(2,1)S(1)}, bf16[33,32,512]{2,1,0:T(8,128)(2,1)S(1)}, u32[]{:S(2)}, u32[]{:S(2)}) collective-permute-start(bf16[33,32,512]{2,1,0:T(8,128)(2,1)S(1)} %get-tuple-element.64), channel_id=1, source_target_pairs={{0,4},{4,0},{8,12},{12,8},{16,20},{20,16},{24,28},{28,24},{1,5},{5... | collective-permute-start | bytes 3244040 | tf_op jit(solution)/shard_map/ppermute | solution.py:424
  33.4 19.6 %collective-permute-start.6 = (bf16[33,8,512]{2,1,0:T(8,128)(2,1)S(1)}, bf16[33,8,512]{2,1,0:T(8,128)(2,1)S(1)}, u32[]{:S(2)}, u32[]{:S(2)}) collective-permute-start(bf16[33,8,512]{2,1,0:T(8,128)(2,1)S(1)} %get-tuple-element.65), channel_id=1, source_target_pairs={{0,1},{1,0},{2,3},{3,2},{4,5},{5,4},{6,7},{7,6},{8,9},{9,8},{10,11... | collective-permute-start | bytes 811016 | tf_op jit(solution)/shard_map/ppermute | solution.py:425
  39.1 13.8 %collective-permute-start.7 = (bf16[33,8,512]{2,1,0:T(8,128)(2,1)S(1)}, bf16[33,8,512]{2,1,0:T(8,128)(2,1)S(1)}, u32[]{:S(2)}, u32[]{:S(2)}) collective-permute-start(bf16[33,8,512]{2,1,0:T(8,128)(2,1)S(1)} %get-tuple-element.66), channel_id=1, source_target_pairs={{1,2},{2,1},{5,6},{6,5},{9,10},{10,9},{13,14},{14,13},{17,18},{18,... | collective-permute-start | bytes 811016 | tf_op jit(solution)/shard_map/ppermute | solution.py:426
  60.8 18.4 %collective-permute-start.8 = (bf16[33,32,512]{2,1,0:T(8,128)(2,1)S(1)}, bf16[33,32,512]{2,1,0:T(8,128)(2,1)S(1)}, u32[]{:S(2)}, u32[]{:S(2)}) collective-permute-start(bf16[33,32,512]{2,1,0:T(8,128)(2,1)S(1)} %get-tuple-element.72), channel_id=1, source_target_pairs={{4,8},{8,4},{12,16},{16,12},{20,24},{24,20},{5,9},{9,5},{13,17},{1... | collective-permute-start | bytes 3244040 | tf_op jit(solution)/shard_map/ppermute | solution.py:423
  61.5 17.6 %collective-permute-start.9 = (bf16[33,32,512]{2,1,0:T(8,128)(2,1)S(1)}, bf16[33,32,512]{2,1,0:T(8,128)(2,1)S(1)}, u32[]{:S(2)}, u32[]{:S(2)}) collective-permute-start(bf16[33,32,512]{2,1,0:T(8,128)(2,1)S(1)} %get-tuple-element.73), channel_id=1, source_target_pairs={{0,4},{4,0},{8,12},{12,8},{16,20},{20,16},{24,28},{28,24},{1,5},{5... | collective-permute-start | bytes 3244040 | tf_op jit(solution)/shard_map/ppermute | solution.py:424
  63.5 15.7 %collective-permute-start.10 = (bf16[33,8,512]{2,1,0:T(8,128)(2,1)S(1)}, bf16[33,8,512]{2,1,0:T(8,128)(2,1)S(1)}, u32[]{:S(2)}, u32[]{:S(2)}) collective-permute-start(bf16[33,8,512]{2,1,0:T(8,128)(2,1)S(1)} %get-tuple-element.74), channel_id=1, source_target_pairs={{0,1},{1,0},{2,3},{3,2},{4,5},{5,4},{6,7},{7,6},{8,9},{9,8},{10,11... | collective-permute-start | bytes 811016 | tf_op jit(solution)/shard_map/ppermute | solution.py:425
  64.1 15.1 %collective-permute-start.11 = (bf16[33,8,512]{2,1,0:T(8,128)(2,1)S(1)}, bf16[33,8,512]{2,1,0:T(8,128)(2,1)S(1)}, u32[]{:S(2)}, u32[]{:S(2)}) collective-permute-start(bf16[33,8,512]{2,1,0:T(8,128)(2,1)S(1)} %get-tuple-element.75), channel_id=1, source_target_pairs={{1,2},{2,1},{5,6},{6,5},{9,10},{10,9},{13,14},{14,13},{17,18},{18,... | collective-permute-start | bytes 811016 | tf_op jit(solution)/shard_map/ppermute | solution.py:426
  86.6 10.0 %all-to-all-start.2 = ((f32[32,1,128]{2,1,0:T(1,128)}), f32[32,1,128]{2,1,0:T(1,128)S(1)}, u32[]{:S(2)}, u32[]{:S(2)}) async-start(f32[32,1,128]{2,1,0:T(1,128)} %bitcast.12), calls=%async_computation.2 | async-start | bytes 32768 | tf_op jit(solution)/shard_map/all_to_all | solution.py:504
